TPU v7x, 32 devices: a whole 2x2x4 slice. The times are simulated.
32 devices in a mesh: seq: 2 (over x), tensor: 4 (over z), bucket: 4 (over y, core).
Axes of the slice: x: 2, y: 2, z: 4, core: 2. Of those that a mesh axis runs over, the one named last changes fastest.
Arguments:
- queries: bfloat16 [4, 1024, 3072], P('bucket', ('seq', 'tensor')), may hold values from -6 to 6
- keys: bfloat16 [4, 1024, 3072], P('bucket', ('seq', 'tensor')), may hold values from -6 to 6
- values: bfloat16 [4, 1024, 3072], P('bucket', ('seq', 'tensor')), may hold values from -6 to 6
- lengths: int32 [4], P('bucket'), may hold values from 256 to 1024, as said below
- out_weight: bfloat16 [3072, 3072], P(('seq', 'bucket'), 'tensor'), may hold values from -0.109375 to 0.109375
Outputs:
- projected: bfloat16 [4, 1024, 3072], P('bucket', ('seq', 'tensor'))
Inputs may be any that keep to these rules, and one draw needn't show every extreme that they name: `lengths`: each bucket has 256 to 1024 live tokens, and at least one bucket has all 1024.
All inputs are finite; a program needn't handle non-finite values.
Results may differ from a plain program's by a relative error of at most 0.018.
Values may be sent and summed in bfloat16 or wider, within the bound.
No kernel may reach another device: no remote copies, remote signals or barrier semaphores. Data moves between devices by JAX's collectives and lax.ppermute only.
A program may use at most 128 MiB of HBM per device.

v0:
```python
import jax
import jax.numpy as jnp
from jax import lax
from jax.sharding import PartitionSpec as P

HS = 128


MASKED_SCORE = -1e30


def shards(queries, keys, values, lengths, out_weight):
    tok_rows = queries.shape[1]
    n_tensor = lax.axis_size("tensor")
    tensor_index = lax.axis_index("tensor")
    live_len = lengths[0]
    local_q, local_k, local_v = (
        lax.all_to_all(queries[0], "seq", split_axis=1, concat_axis=0, tiled=True),
        lax.all_to_all(keys[0], "seq", split_axis=1, concat_axis=0, tiled=True),
        lax.all_to_all(values[0], "seq", split_axis=1, concat_axis=0, tiled=True),
    )
    row_count, col_count = local_q.shape
    head_count = col_count // HS
    query_heads = local_q.reshape(row_count, head_count, HS)

    def spots(first_row, total_rows):
        index_row = first_row + jnp.arange(total_rows, dtype=jnp.int32)
        owner = index_row // row_count
        within = index_row % row_count
        return (within // tok_rows * n_tensor + owner) * tok_rows + within % tok_rows

    query_usable = spots(tensor_index * row_count, row_count) < live_len
    initial = (
        jnp.full((row_count, head_count), MASKED_SCORE, jnp.float32),
        jnp.zeros((row_count, head_count), jnp.float32),
        jnp.zeros((row_count, head_count, HS), jnp.float32),
    )
    carried = initial
    first_row = jnp.int32(0)
    key_rows = lax.all_gather(local_k, "tensor", axis=0, tiled=True)
    value_rows = lax.all_gather(local_v, "tensor", axis=0, tiled=True)
    for offset in range(key_rows.shape[0] // row_count):
        row_peak, row_sum, accumulated = carried
        key_tile = key_rows[offset * row_count : (offset + 1) * row_count].reshape(
            row_count, head_count, HS
        )
        value_tile = value_rows[offset * row_count : (offset + 1) * row_count].reshape(
            row_count, head_count, HS
        )
        key_usable = spots(first_row + offset * row_count, row_count) < live_len
        scores = jnp.einsum(
            "qhd,khd->qhk", query_heads, key_tile, preferred_element_type=jnp.float32
        ) * HS ** (-0.5)
        scores = jnp.where(key_usable[None, None, :], scores, MASKED_SCORE)
        peak_new = jnp.maximum(row_peak, jnp.max(scores, axis=-1))
        exponent = jnp.where(key_usable[None, None, :], jnp.exp(scores - peak_new[..., None]), 0.0)
        rescale = jnp.exp(row_peak - peak_new)
        accumulated = accumulated * rescale[..., None] + jnp.einsum(
            "qhk,khd->qhd",
            exponent.astype(jnp.bfloat16),
            value_tile,
            preferred_element_type=jnp.float32,
        )
        carried = (peak_new, row_sum * rescale + jnp.sum(exponent, axis=-1), accumulated)
    row_peak, row_sum, accumulated = carried
    attended = accumulated / row_sum[..., None]
    mixed = jnp.where(query_usable[:, None], attended.reshape(row_count, col_count), 0.0).astype(
        jnp.bfloat16
    )
    restored = lax.all_to_all(mixed, "seq", split_axis=0, concat_axis=1, tiled=True)
    wide_weight = lax.all_gather(out_weight, "tensor", axis=1, tiled=True)
    summed = jnp.dot(
        restored,
        lax.all_gather(wide_weight, ("seq", "bucket"), axis=0, tiled=True),
        preferred_element_type=jnp.float32,
    )
    return summed.astype(jnp.bfloat16)[None]


def solution(mesh):
    in_specs = (
        P("bucket", ("seq", "tensor"), None),
        P("bucket", ("seq", "tensor"), None),
        P("bucket", ("seq", "tensor"), None),
        P("bucket"),
        P(("seq", "bucket"), "tensor"),
    )
    out_specs = P("bucket", ("seq", "tensor"), None)
    return jax.shard_map(shards, mesh=mesh, in_specs=in_specs, out_specs=out_specs, check_vma=False)
```

profile of v0, /device:TPU:0, one launch (start us, length us, event | category | flops | bytes accessed | tf_op | source)
XLA Modules:
  0.0 309.9 jit_solution(5005568359367810147)
XLA Ops:
  6.5 0.7 all-gather.9.cloned.1.call-update
  7.3 0.0 all-gather.5.cloned.1.call-start
  7.3 1.5 copy.68
  8.8 14.8 %all_to_all.70 = bf16[128,2,1536]{0,2,1:T(8,128)(2,1)S(1)} all-to-all(bf16[128,2,1536]{0,2,1:T(8,128)(2,1)S(1)} %bitcast.125), channel_id=1, replica_groups=mesh['seq'=2,'tensor'=4,'bucket'=4] {'seq'}, dimensions={1} | all-to-all | bytes 1572864 | tf_op jit(solution)/shard_map/all_to_all | solution.py:19
  23.6 1.2 copy.69
  24.8 0.0 all-gather.5.cloned.1.call-update
  24.8 0.0 all-gather.7.cloned.1.call-start
  24.9 0.4 copy.75
  25.3 12.5 %all_to_all.71 = bf16[128,2,1536]{0,2,1:T(8,128)(2,1)S(1)} all-to-all(bf16[128,2,1536]{0,2,1:T(8,128)(2,1)S(1)} %bitcast.126), channel_id=1, replica_groups=mesh['seq'=2,'tensor'=4,'bucket'=4] {'seq'}, dimensions={1} | all-to-all | bytes 1572864 | tf_op jit(solution)/shard_map/all_to_all | solution.py:20
  37.8 1.2 copy.76
  39.0 0.0 all-gather.11.cloned.1.call-start
  39.0 22.6 %all-gather.9.cloned.1.call-done = bf16[384,3072]{1,0:T(8,128)(2,1)} async-done(((bf16[384,768]{1,0:T(8,128)(2,1)}), bf16[384,3072]{1,0:T(8,128)(2,1)}) %all-gather.9.cloned.1.call-update) | async-done | bytes 2359312 | tf_op jit(solution)/shard_map/all_gather | solution.py:71
  61.7 1.2 copy.71
  62.8 3.5 %all-to-all-start.1 = ((bf16[128,2,1536]{0,2,1:T(8,128)(2,1)}), bf16[128,2,1536]{0,2,1:T(8,128)(2,1)S(1)}, u32[]{:S(2)}, u32[]{:S(2)}) async-start(bf16[128,2,1536]{0,2,1:T(8,128)(2,1)} %bitcast.5), calls=%async_computation.1 | async-start | bytes 1572864 | tf_op jit(solution)/shard_map/all_to_all | solution.py:18
  67.1 10.2 %all-to-all-done.1 = bf16[128,2,1536]{0,2,1:T(8,128)(2,1)S(1)} async-done(((bf16[128,2,1536]{0,2,1:T(8,128)(2,1)}), bf16[128,2,1536]{0,2,1:T(8,128)(2,1)S(1)}, u32[]{:S(2)}, u32[]{:S(2)}) %all-to-all-start.1) | async-done | bytes 786464 | tf_op jit(solution)/shard_map/all_to_all | solution.py:18
  77.3 6.7 %copy.72 = bf16[2,128,1536]{1,0,2:T(2,128)(2,1)S(1)} copy(bf16[2,128,1536]{1,2,0:T(8,128)(2,1)S(1)} %bitcast.122) | data formatting | bytes 1572864 | tf_op jit(solution)/shard_map/all_to_all | solution.py:18
  83.9 0.5 reshape.424
  84.4 41.0 %all-gather.5.cloned.1.call-done = bf16[1024,1536]{1,0:T(8,128)(2,1)} async-done(((bf16[256,1536]{1,0:T(8,128)(2,1)}), bf16[1024,1536]{1,0:T(8,128)(2,1)}) %all-gather.5.cloned.1.call-update) | async-done | bytes 3145744 | tf_op jit(solution)/shard_map/all_gather | solution.py:40
  125.4 2.9 fusion.89
  128.4 1.2 copy.70
  129.6 0.3 copy.92
  129.8 0.3 copy.86
  130.1 1.4 copy.80
  131.5 57.6 %all-gather.7.cloned.1.call-done = bf16[1024,1536]{1,0:T(8,128)(2,1)} async-done(((bf16[256,1536]{1,0:T(8,128)(2,1)}), bf16[1024,1536]{1,0:T(8,128)(2,1)}) %all-gather.7.cloned.1.call-update) | async-done | bytes 3145744 | tf_op jit(solution)/shard_map/all_gather | solution.py:41
  189.1 3.6 %fusion.88 = (bf16[256,1536]{1,0:T(8,128)(2,1)}, bf16[256,1536]{1,0:T(8,128)(2,1)}, bf16[256,1536]{1,0:T(8,128)(2,1)}, bf16[256,1536]{1,0:T(8,128)(2,1)}) fusion(bf16[1024,1536]{1,0:T(8,128)(2,1)} %all-gather.7.cloned.1.call-done), kind=kLoop, calls=%fused_computation.155 | loop fusion | bytes 6291456 | tf_op jit(solution)/shard_map/slice | solution.py:47
  192.7 2.3 copy.83
  195.0 2.5 copy.89
  197.5 2.4 copy.95
  199.9 2.5 copy.77
  202.4 1.9 bitcast_reduce_fusion.3
  204.3 0.8 bitcast_reduce_fusion
  205.2 0.8 bitcast_reduce_fusion.1
  206.1 0.8 bitcast_reduce_fusion.2
  206.9 0.8 fusion.11
  207.8 0.8 fusion.13
  208.6 0.8 fusion.15
  209.5 0.8 fusion.9
  210.4 1.2 fusion.21
  211.6 1.4 fusion.19
  212.9 1.2 fusion.17
  214.2 3.0 fusion.25
  217.2 0.3 copy.98
  217.5 0.2 reshape.432
  217.7 0.8 select_convert_fusion
  218.4 0.1 copy.99
  218.6 16.7 %all_to_all.72 = bf16[2,128,1536]{1,2,0:T(8,128)(2,1)S(1)} all-to-all(bf16[2,128,1536]{1,2,0:T(8,128)(2,1)S(1)} %copy.99), channel_id=1, replica_groups=mesh['seq'=2,'tensor'=4,'bucket'=4] {'seq'}, dimensions={0} | all-to-all | bytes 1572864 | tf_op jit(solution)/shard_map/all_to_all | solution.py:70
  235.3 58.3 %all-gather.11.cloned.1.call-done = bf16[3072,3072]{1,0:T(8,128)(2,1)} async-done(((bf16[384,3072]{1,0:T(8,128)(2,1)}), bf16[3072,3072]{1,0:T(8,128)(2,1)}) %all-gather.11.cloned.1.call-update) | async-done | bytes 18874384 | tf_op jit(solution)/shard_map/all_gather | solution.py:74
  293.5 9.9 %fusion = bf16[1,128,3072]{2,1,0:T(8,128)(2,1)} fusion(bf16[128,3072]{0,1:T(8,128)(2,1)S(1)} %bitcast.115, bf16[3072,3072]{1,0:T(8,128)(2,1)} %all-gather.11.cloned.1.call-done), kind=kOutput, calls=%fused_computation.1 | convolution fusion | flops 2416312320 | bytes 20447232 | tf_op jit(solution)/shard_map/dot_general | solution.py:72
  (20 shorter events, 0.2 us)
Async XLA Ops:
  6.5 18.3 %copy-start = (bf16[1,128,3072]{2,1,0:T(8,128)(2,1)S(1)}, bf16[1,128,3072]{2,1,0:T(8,128)(2,1)}, u32[]{:S(2)}) copy-start(bf16[1,128,3072]{2,1,0:T(8,128)(2,1)} %param.7) | copy-start | bytes 2359300
  6.5 55.1 %all-gather.9.cloned.1.call-start = ((), (), s32[]{:S(2)}) async-start(), calls=%async_computation.6 | async-start | bytes 2949120 | tf_op jit(solution)/shard_map/all_gather | solution.py:71
  7.3 118.2 %all-gather.5.cloned.1.call-start = ((), (), s32[]{:S(2)}) async-start(), calls=%async_computation.4 | async-start | bytes 3932160 | tf_op jit(solution)/shard_map/all_gather | solution.py:40
  24.8 164.3 %all-gather.7.cloned.1.call-start = ((), (), s32[]{:S(2)}) async-start(), calls=%async_computation.5 | async-start | bytes 3932160 | tf_op jit(solution)/shard_map/all_gather | solution.py:41
  25.3 36.4 %copy-start.1 = (bf16[1,128,3072]{2,1,0:T(8,128)(2,1)S(1)}, bf16[1,128,3072]{2,1,0:T(8,128)(2,1)}, u32[]{:S(2)}) copy-start(bf16[1,128,3072]{2,1,0:T(8,128)(2,1)} %param.5) | copy-start | bytes 2359300
  39.0 254.6 %all-gather.11.cloned.1.call-start = ((), (), s32[]{:S(2)}) async-start(), calls=%async_computation.7 | async-start | bytes 21233664 | tf_op jit(solution)/shard_map/all_gather | solution.py:74
  62.8 14.4 %all-to-all-start.1 = ((bf16[128,2,1536]{0,2,1:T(8,128)(2,1)}), bf16[128,2,1536]{0,2,1:T(8,128)(2,1)S(1)}, u32[]{:S(2)}, u32[]{:S(2)}) async-start(bf16[128,2,1536]{0,2,1:T(8,128)(2,1)} %bitcast.5), calls=%async_computation.1 | async-start | bytes 1572864 | tf_op jit(solution)/shard_map/all_to_all | solution.py:18
  208.6 1.7 copy-start.5
  210.4 1.2 copy-start.4
  211.6 1.4 copy-start.3
  212.9 1.2 copy-start.2
Sparse Core Ops, SparseCore 0:
  8.9 52.6 all-gather.8
  63.2 62.1 all-gather.4
  127.0 62.0 all-gather.6
  190.9 102.6 all-gather.10
where the time goes:
time: 311 us; the launch traced here: 310 us
  waiting for transfers between devices  190 us (61%)
  blocking collectives  44 us (14%)
  local copies, waits for them, and re-layouts  32.5 us (10%)
  matrix products  21.1 us (7%)
  between operations  14.1 us (5%)
  other arithmetic  4.22 us (1%)
  starting transfers between devices  3.66 us (1%)
    all_gather x1, waiting for transfers between devices, shards(): lax.all_gather(wide_weight, ('seq', 'bucket'), axis=0, tiled=True)  58.3 us
    all_gather x1, waiting for transfers between devices, shards(): value_rows = lax.all_gather(local_v, 'tensor', axis=0, tiled=True)  57.6 us
    all_gather x1, waiting for transfers between devices, shards(): key_rows = lax.all_gather(local_k, 'tensor', axis=0, tiled=True)  41 us
    all_gather x1, waiting for transfers between devices, shards(): wide_weight = lax.all_gather(out_weight, 'tensor', axis=1, tiled=True)  22.6 us
    all_to_all x1, blocking collectives, shards(): lax.all_to_all(mixed, 'seq', split_axis=0, concat_axis=1, tiled=True)  16.7 us
    all_to_all x1, blocking collectives, shards(): lax.all_to_all(keys[0], 'seq', split_axis=1, concat_axis=0, tiled=True)  14.8 us
    slice x5, local copies, waits for them, and re-layouts, shards(): value_rows[offset * row_count:(offset + 1) * row_count]  13.3 us
    all_to_all x1, blocking collectives, shards(): lax.all_to_all(values[0], 'seq', split_axis=1, concat_axis=0, tiled=True)  12.5 us
  transfers between devices with their start and end apart: 5, of which 5 were waited for; matrix products, arithmetic and copies ran while one was open for 15% of the time, Pallas kernels for 0%

commit v1 on v0

--- a/solution.py
+++ b/solution.py
@@ -1,12 +1,22 @@
+import functools
+import math
+
 import jax
 import jax.numpy as jnp
 from jax import lax
+from jax.experimental import pallas as pl
+from jax.experimental.pallas import tpu as pltpu
 from jax.sharding import PartitionSpec as P
 
 HS = 128
+LOG2E = math.log2(math.e)
 
 
 MASKED_SCORE = -1e30
+
+TOKENS = P("bucket", ("seq", "tensor"), None)
+IN_SPECS = (TOKENS, TOKENS, TOKENS, P("bucket"), P(("seq", "bucket"), "tensor"))
+OUT_SPECS = TOKENS
 
 
 def shards(queries, keys, values, lengths, out_weight):
@@ -77,13 +87,159 @@
     return summed.astype(jnp.bfloat16)[None]
 
 
+def pack_kernel(dest_ref, q_ref, k_ref, v_ref, *out_refs):
+    width = out_refs[0].shape[-1]
+    for j, out_ref in enumerate(out_refs):
+        cols = pl.ds(pl.multiple_of(dest_ref[j] * width, HS), width)
+        out_ref[0] = q_ref[:, cols]
+        out_ref[1] = k_ref[:, cols]
+        out_ref[2] = v_ref[:, cols]
+
+
+def attend_kernel(pos_ref, *refs, n_seq, n_tensor):
+    groups = n_seq * n_tensor
+    blocks, outs = refs[:groups], refs[groups : groups + n_tensor]
+    k_scr, v_scr = refs[groups + n_tensor :]
+    rows, width = blocks[0].shape[1:]
+    live_len = pos_ref[groups]
+    for h in range(width // HS):
+        for j in range(groups):
+            k_scr[h, j * rows : (j + 1) * rows, :] = blocks[j][1, :, h * HS : (h + 1) * HS]
+            v_scr[h, j * rows : (j + 1) * rows, :] = blocks[j][2, :, h * HS : (h + 1) * HS]
+    spot = lax.broadcasted_iota(jnp.int32, (1, rows), 1)
+    bias = jnp.concatenate(
+        [jnp.where(pos_ref[j] + spot < live_len, 0.0, MASKED_SCORE) for j in range(groups)], axis=1
+    )
+    row_spot = lax.broadcasted_iota(jnp.int32, (rows, HS), 0)
+    for h in range(width // HS):
+        cols = slice(h * HS, (h + 1) * HS)
+        for j in range(groups):
+            scores = lax.dot_general(
+                blocks[j][0, :, cols], k_scr[h], (((1,), (1,)), ((), ())),
+                preferred_element_type=jnp.float32,
+            ) + bias
+            peak = jnp.max(scores, axis=-1, keepdims=True)
+            expo = jnp.exp2((scores - peak) * (HS ** -0.5 * LOG2E))
+            total = jnp.sum(expo, axis=-1, keepdims=True)
+            mixed = jnp.dot(expo.astype(jnp.bfloat16), v_scr[h], preferred_element_type=jnp.float32)
+            mixed = jnp.where(pos_ref[j] + row_spot < live_len, mixed / total, 0.0)
+            outs[j % n_tensor][j // n_tensor, :, cols] = mixed.astype(jnp.bfloat16)
+
+
+def project_kernel(where_ref, *refs, row_set, n_tensor, n_bucket):
+    pieces, weights = refs[:n_tensor], refs[n_tensor : n_tensor + n_bucket * n_tensor]
+    out_ref, o_scr = refs[n_tensor + n_bucket * n_tensor :]
+    width = weights[0].shape[1]
+    z, b = where_ref[0], where_ref[1]
+    for dz in range(n_tensor):
+        o_scr[lax.rem(z + dz, n_tensor)] = pieces[dz][row_set]
+    for dz in range(n_tensor):
+        acc = None
+        for m in range(n_bucket):
+            part = jnp.dot(
+                o_scr[jnp.bitwise_xor(b, m)], weights[m * n_tensor + dz][...],
+                preferred_element_type=jnp.float32,
+            )
+            acc = part if acc is None else acc + part
+        place = pl.multiple_of(lax.rem(z - dz + n_tensor, n_tensor) * width, HS)
+        out_ref[:, pl.ds(place, width)] = acc.astype(out_ref.dtype)
+
+
+def vmem_call(kernel, n_in, out_shape, scratch=(), name=None):
+    vmem = pl.BlockSpec(memory_space=pltpu.VMEM)
+    return pl.pallas_call(
+        kernel,
+        in_specs=[pl.BlockSpec(memory_space=pltpu.SMEM)] + [vmem] * n_in,
+        out_specs=[vmem] * len(out_shape),
+        out_shape=out_shape,
+        scratch_shapes=scratch,
+        name=name,
+    )
+
+
+def head_shards(queries, keys, values, lengths, out_weight):
+    n_seq, n_tensor, n_bucket = (lax.axis_size(a) for a in ("seq", "tensor", "bucket"))
+    s, z, b = (lax.axis_index(a).astype(jnp.int32) for a in ("seq", "tensor", "bucket"))
+    groups = n_seq * n_tensor
+    rows, model = queries.shape[1:]
+    width = model // groups
+    bf16, f32 = jnp.bfloat16, jnp.float32
+    shifts = [(ds, dz) for ds in range(n_seq) for dz in range(n_tensor)]
+
+    dest = jnp.stack([(s + ds) % n_seq * n_tensor + (z + dz) % n_tensor for ds, dz in shifts])
+    packed = vmem_call(
+        pack_kernel, 3, [jax.ShapeDtypeStruct((3, rows, width), bf16)] * groups, name="pack"
+    )(dest, queries[0], keys[0], values[0])
+
+    def shifted(x, ds, dz):
+        perm = [
+            (i * n_tensor + t, (i + ds) % n_seq * n_tensor + (t + dz) % n_tensor)
+            for i in range(n_seq)
+            for t in range(n_tensor)
+        ]
+        return lax.ppermute(x, ("seq", "tensor"), perm)
+
+    blocks = [packed[0]] + [shifted(packed[j], *shifts[j]) for j in range(1, groups)]
+
+    weights = [out_weight]
+    for dz in range(1, n_tensor):
+        weights.append(shifted(out_weight, 0, dz))
+    bit = n_bucket // 2
+    held = {0: weights}
+    while bit:
+        swap = [(i, i ^ bit) for i in range(n_bucket)]
+        held.update(
+            {m ^ bit: [lax.ppermute(w, "bucket", swap) for w in held[m]] for m in list(held)}
+        )
+        bit //= 2
+    flat_weights = [w for m in range(n_bucket) for w in held[m]]
+
+    pos = jnp.stack(
+        [((s - ds) % n_seq * n_tensor + (z - dz) % n_tensor) * rows for ds, dz in shifts]
+        + [lengths[0]]
+    )
+    mixed = vmem_call(
+        functools.partial(attend_kernel, n_seq=n_seq, n_tensor=n_tensor),
+        groups,
+        [jax.ShapeDtypeStruct((n_seq, rows, width), bf16)] * n_tensor,
+        [pltpu.VMEM((width // HS, groups * rows, HS), bf16)] * 2,
+        name="attend",
+    )(pos, *blocks)
+    pieces = [mixed[0]] + [shifted(mixed[dz], 0, -dz) for dz in range(1, n_tensor)]
+
+    def project(row_set, dtype):
+        return vmem_call(
+            functools.partial(
+                project_kernel, row_set=row_set, n_tensor=n_tensor, n_bucket=n_bucket
+            ),
+            n_tensor + n_tensor * n_bucket,
+            [jax.ShapeDtypeStruct((rows, model), dtype)],
+            [pltpu.VMEM((n_tensor, rows, width), bf16)],
+            name=f"project{row_set}",
+        )(jnp.stack([z, b]), *pieces, *flat_weights)[0]
+
+    received = [
+        shifted(project(ds, bf16), -ds, 0) for ds in range(1, n_seq)
+    ]
+    summed = project(0, f32)
+    for other in received:
+        summed = summed + other.astype(f32)
+    return summed.astype(bf16)[None]
+
+
 def solution(mesh):
-    in_specs = (
-        P("bucket", ("seq", "tensor"), None),
-        P("bucket", ("seq", "tensor"), None),
-        P("bucket", ("seq", "tensor"), None),
-        P("bucket"),
-        P(("seq", "bucket"), "tensor"),
-    )
-    out_specs = P("bucket", ("seq", "tensor"), None)
-    return jax.shard_map(shards, mesh=mesh, in_specs=in_specs, out_specs=out_specs, check_vma=False)
+    n_seq, n_tensor, n_bucket = (mesh.shape[a] for a in ("seq", "tensor", "bucket"))
+
+    def run(queries, keys, values, lengths, out_weight):
+        heads = queries.shape[2] // HS
+        by_head = (
+            heads % (n_seq * n_tensor) == 0
+            and n_tensor == n_bucket
+            and n_bucket & (n_bucket - 1) == 0
+        )
+        return jax.shard_map(
+            head_shards if by_head else shards,
+            mesh=mesh, in_specs=IN_SPECS, out_specs=OUT_SPECS, check_vma=False,
+        )(queries, keys, values, lengths, out_weight)
+
+    return run

time: 311 us -> 204 us (0.66)
  waiting for transfers between devices: 190 us -> 107 us
  starting transfers between devices: 3.66 us -> 62.6 us
  blocking collectives: 44 us -> 0 us
  local copies, waits for them, and re-layouts: 32.5 us -> 2.38 us
  Pallas kernels: 0 us -> 28 us
  matrix products: 21.1 us -> 0 us
  between operations: 14.1 us -> 0.83 us
    all_gather x4 -> x0, waiting for transfers between devices: 180 us -> none  [the longest x1 58.3 us: shards(): lax.all_gather(wide_weight, ('seq', 'bucket'), axis=0, tiled=True)]
    ppermute x0 -> x26, waiting for transfers between devices: none -> 107 us  [the longest x14 78.3 us: shifted(): return lax.ppermute(x, ('seq', 'tensor'), perm)]
    ppermute x0 -> x26, starting transfers between devices: none -> 62.6 us  [the longest x14 56 us: shifted(): return lax.ppermute(x, ('seq', 'tensor'), perm)]
    all_to_all x3 -> x0, blocking collectives: 44 us -> none  [the longest x1 16.7 us: shards(): lax.all_to_all(mixed, 'seq', split_axis=0, concat_axis=1, tiled=True)]
    pallas_call x0 -> x4, Pallas kernels: none -> 28 us  [the longest x2 13.6 us: project(): vmem_call(functools.partial(project_kernel, row_set=row_set, n_tensor=n_t...]
    dot_general x9 -> x0, matrix products: 21.1 us -> none  [the longest x1 9.88 us: shards(): jnp.dot(restored, lax.all_gather(wide_weight, ('seq', 'bucket'), axis=0,...]
    slice x10 -> x0, local copies, waits for them, and re-layouts: 19.3 us -> none  [the longest x5 13.3 us: shards(): value_rows[offset * row_count:(offset + 1) * row_count]]
    all_to_all x1 -> x0, waiting for transfers between devices: 10.2 us -> none  [shards(): lax.all_to_all(queries[0], 'seq', split_axis=1, concat_axis=0, tiled=True)]
  transfers between devices with their start and end apart: 5 -> 26, of which waited for: 5 -> 14; matrix products, arithmetic and copies ran while one was open for 15% -> 1% of each run, Pallas kernels for 0% -> 3%
where the time goes in v1:
time: 204 us
  waiting for transfers between devices  107 us (52%)
  starting transfers between devices  62.6 us (31%)
  Pallas kernels  28 us (14%)
  other arithmetic  3.09 us (2%)
  local copies, waits for them, and re-layouts  2.38 us (1%)
    ppermute x14, waiting for transfers between devices, shifted(): return lax.ppermute(x, ('seq', 'tensor'), perm)  78.3 us
    ppermute x14, starting transfers between devices, shifted(): return lax.ppermute(x, ('seq', 'tensor'), perm)  56 us
    ppermute x12, waiting for transfers between devices, head_shards(): lax.ppermute(w, 'bucket', swap)  28.6 us
    pallas_call x2, Pallas kernels, project(): vmem_call(functools.partial(project_kernel, row_set=row_set, n_tensor=n_t...  13.6 us
    pallas_call x1, Pallas kernels, head_shards(): vmem_call(functools.partial(attend_kernel, n_seq=n_seq, n_tensor=n_tensor...  11.1 us
    ppermute x12, starting transfers between devices, head_shards(): lax.ppermute(w, 'bucket', swap)  6.63 us
  transfers between devices with their start and end apart: 26, of which 14 were waited for; matrix products, arithmetic and copies ran while one was open for 1% of the time, Pallas kernels for 3%

profile of v1, /device:TPU:0, one launch (start us, length us, event | category | flops | bytes accessed | tf_op | source)
XLA Modules:
  0.0 203.8 jit_solution(14396957859359637679)
XLA Ops:
  0.0 0.7 stack.86.dest_ref
  0.7 3.2 %pack.1 = (bf16[3,128,384]{2,1,0:T(8,128)(2,1)}, bf16[3,128,384]{2,1,0:T(8,128)(2,1)}, bf16[3,128,384]{2,1,0:T(8,128)(2,1)}, bf16[3,128,384]{2,1,0:T(8,128)(2,1)...) custom-call(s32[8]{0:T(128)} %stack.86.dest_ref, ...), custom_call_target="tpu_custom_call" | custom-call | tf_op jit(solution)/shard_map/pack/pallas_call | solution.py:170
  3.9 3.1 %collective-permute-start = (bf16[3,128,384]{2,1,0:T(8,128)(2,1)}, bf16[3,128,384]{2,1,0:T(8,128)(2,1)S(1)}, u32[]{:S(2)}, u32[]{:S(2)}) collective-permute-start(bf16[3,128,384]{2,1,0:T(8,128)(2,1)} %get-tuple-element.18), channel_id=1, source_target_pairs={{0,4},{4,8},{8,12},{12,0},{16,20},{20,24},{24,28},{28,16},{1,5},{5... | collective-permute-start | bytes 884744 | tf_op jit(solution)/shard_map/ppermute | solution.py:180
  7.0 2.6 %collective-permute-start.1 = (bf16[3,128,384]{2,1,0:T(8,128)(2,1)}, bf16[3,128,384]{2,1,0:T(8,128)(2,1)S(1)}, u32[]{:S(2)}, u32[]{:S(2)}) collective-permute-start(bf16[3,128,384]{2,1,0:T(8,128)(2,1)} %get-tuple-element.19), channel_id=1, source_target_pairs={{0,8},{4,12},{8,0},{12,4},{16,24},{20,28},{24,16},{28,20},{1,9},{5... | collective-permute-start | bytes 884744 | tf_op jit(solution)/shard_map/ppermute | solution.py:180
  9.6 1.3 collective-permute-start.2
  10.9 1.5 collective-permute-start.3
  12.4 0.6 collective-permute-start.4
  13.1 4.2 %collective-permute-done.refs_1_ = bf16[3,128,384]{2,1,0:T(8,128)(2,1)S(1)} collective-permute-done((bf16[3,128,384]{2,1,0:T(8,128)(2,1)}, bf16[3,128,384]{2,1,0:T(8,128)(2,1)S(1)}, u32[]{:S(2)}, u32[]{:S(2)}) %collective-permute-start) | collective-permute-done | bytes 294944 | tf_op jit(solution)/shard_map/ppermute | solution.py:180
  17.2 14.5 %collective-permute-start.5 = (bf16[3,128,384]{2,1,0:T(8,128)(2,1)}, bf16[3,128,384]{2,1,0:T(8,128)(2,1)S(1)}, u32[]{:S(2)}, u32[]{:S(2)}) collective-permute-start(bf16[3,128,384]{2,1,0:T(8,128)(2,1)} %get-tuple-element.23), channel_id=1, source_target_pairs={{0,24},{4,28},{8,16},{12,20},{16,8},{20,12},{24,0},{28,4},{1,25},{... | collective-permute-start | bytes 884744 | tf_op jit(solution)/shard_map/ppermute | solution.py:180
  31.7 0.0 collective-permute-done.1.refs_2_
  31.7 16.7 %collective-permute-start.6 = (bf16[3,128,384]{2,1,0:T(8,128)(2,1)}, bf16[3,128,384]{2,1,0:T(8,128)(2,1)S(1)}, u32[]{:S(2)}, u32[]{:S(2)}) collective-permute-start(bf16[3,128,384]{2,1,0:T(8,128)(2,1)} %get-tuple-element.24), channel_id=1, source_target_pairs={{0,28},{4,16},{8,20},{12,24},{16,12},{20,0},{24,4},{28,8},{1,29},{... | collective-permute-start | bytes 884744 | tf_op jit(solution)/shard_map/ppermute | solution.py:180
  49.0 0.6 stack.77.pos_ref
  49.7 0.0 collective-permute-done.2.refs_3_
  49.7 5.5 %collective-permute-done.5.refs_6_ = bf16[3,128,384]{2,1,0:T(8,128)(2,1)S(1)} collective-permute-done((bf16[3,128,384]{2,1,0:T(8,128)(2,1)}, bf16[3,128,384]{2,1,0:T(8,128)(2,1)S(1)}, u32[]{:S(2)}, u32[]{:S(2)}) %collective-permute-start.5) | collective-permute-done | bytes 294944 | tf_op jit(solution)/shard_map/ppermute | solution.py:180
  55.3 1.7 collective-permute-done.6.refs_7_
  57.0 0.7 copy-done.17
  57.7 11.1 %attend.1 = (bf16[2,128,384]{2,1,0:T(8,128)(2,1)}, bf16[2,128,384]{2,1,0:T(8,128)(2,1)}, bf16[2,128,384]{2,1,0:T(8,128)(2,1)}, bf16[2,128,384]{2,1,0:T(8,128)(2,1)}) custom-call(s32[9]{0:T(128)} %stack.77.pos_ref, bf16[3,128,384]{2,1,0:T(8,128)(2,1)} %get-tuple-element.17.refs_0_, bf16[3,128,384]{2,1,0:T(8,128)(2,1)} %copy-done.11, ...), custom_call_target="tpu_custom_call" | custom-call | tf_op jit(solution)/shard_map/attend/pallas_call | solution.py:201
  68.8 6.3 %collective-permute-start.7 = (bf16[2,128,384]{2,1,0:T(8,128)(2,1)}, bf16[2,128,384]{2,1,0:T(8,128)(2,1)S(1)}, u32[]{:S(2)}, u32[]{:S(2)}) collective-permute-start(bf16[2,128,384]{2,1,0:T(8,128)(2,1)} %get-tuple-element.26), channel_id=1, source_target_pairs={{0,12},{4,0},{8,4},{12,8},{16,28},{20,16},{24,20},{28,24},{1,13},{... | collective-permute-start | bytes 589832 | tf_op jit(solution)/shard_map/ppermute | solution.py:180
  75.1 0.3 collective-permute-start.8
  75.4 0.3 collective-permute-start.9
  75.7 2.9 %collective-permute-start.10 = (bf16[384,768]{1,0:T(8,128)(2,1)S(1)}, bf16[384,768]{1,0:T(8,128)(2,1)S(1)}, u32[]{:S(2)}, u32[]{:S(2)}) collective-permute-start(bf16[384,768]{1,0:T(8,128)(2,1)S(1)} %copy-done), channel_id=1, source_target_pairs={{0,4},{4,8},{8,12},{12,0},{16,20},{20,24},{24,28},{28,16},{1,5},{5... | collective-permute-start | bytes 1769480 | tf_op jit(solution)/shard_map/ppermute | solution.py:180
  78.6 1.2 collective-permute-start.11
  79.8 1.0 collective-permute-done.7.refs_1_
  80.7 4.2 %collective-permute-start.12 = (bf16[384,768]{1,0:T(8,128)(2,1)S(1)}, bf16[384,768]{1,0:T(8,128)(2,1)S(1)}, u32[]{:S(2)}, u32[]{:S(2)}) collective-permute-start(bf16[384,768]{1,0:T(8,128)(2,1)S(1)} %copy-done), channel_id=1, source_target_pairs={{0,12},{4,0},{8,4},{12,8},{16,28},{20,16},{24,20},{28,24},{1,13},{... | collective-permute-start | bytes 1769480 | tf_op jit(solution)/shard_map/ppermute | solution.py:180
  85.0 34.4 %collective-permute-done.8.refs_2_ = bf16[2,128,384]{2,1,0:T(8,128)(2,1)S(1)} collective-permute-done((bf16[2,128,384]{2,1,0:T(8,128)(2,1)}, bf16[2,128,384]{2,1,0:T(8,128)(2,1)S(1)}, u32[]{:S(2)}, u32[]{:S(2)}) %collective-permute-start.8) | collective-permute-done | bytes 196640 | tf_op jit(solution)/shard_map/ppermute | solution.py:180
  119.4 1.5 collective-permute-start.17
  120.9 0.6 collective-permute-start.18
  121.5 10.5 %collective-permute-done.11.refs_6_ = bf16[384,768]{1,0:T(8,128)(2,1)S(1)} collective-permute-done((bf16[384,768]{1,0:T(8,128)(2,1)S(1)}, bf16[384,768]{1,0:T(8,128)(2,1)S(1)}, u32[]{:S(2)}, u32[]{:S(2)}) %collective-permute-start.11) | collective-permute-done | bytes 589856 | tf_op jit(solution)/shard_map/ppermute | solution.py:180
  131.9 1.5 collective-permute-start.19
  133.5 8.7 %collective-permute-done.12.refs_7_ = bf16[384,768]{1,0:T(8,128)(2,1)S(1)} collective-permute-done((bf16[384,768]{1,0:T(8,128)(2,1)S(1)}, bf16[384,768]{1,0:T(8,128)(2,1)S(1)}, u32[]{:S(2)}, u32[]{:S(2)}) %collective-permute-start.12) | collective-permute-done | bytes 589856 | tf_op jit(solution)/shard_map/ppermute | solution.py:180
  142.2 1.4 collective-permute-start.20
  143.7 0.1 collective-permute-start.14
  143.8 0.5 collective-permute-start.15
  144.3 4.0 %collective-permute-done.18.refs_13_ = bf16[384,768]{1,0:T(8,128)(2,1)} collective-permute-done((bf16[384,768]{1,0:T(8,128)(2,1)S(1)}, bf16[384,768]{1,0:T(8,128)(2,1)}, u32[]{:S(2)}, u32[]{:S(2)}) %collective-permute-start.18) | collective-permute-done | bytes 589856 | tf_op jit(solution)/shard_map/ppermute | solution.py:192
  148.3 12.6 %collective-permute-done.19.refs_14_ = bf16[384,768]{1,0:T(8,128)(2,1)} collective-permute-done((bf16[384,768]{1,0:T(8,128)(2,1)S(1)}, bf16[384,768]{1,0:T(8,128)(2,1)}, u32[]{:S(2)}, u32[]{:S(2)}) %collective-permute-start.19) | collective-permute-done | bytes 589856 | tf_op jit(solution)/shard_map/ppermute | solution.py:192
  160.9 9.9 %collective-permute-done.20.refs_15_ = bf16[384,768]{1,0:T(8,128)(2,1)} collective-permute-done((bf16[384,768]{1,0:T(8,128)(2,1)S(1)}, bf16[384,768]{1,0:T(8,128)(2,1)}, u32[]{:S(2)}, u32[]{:S(2)}) %collective-permute-start.20) | collective-permute-done | bytes 589856 | tf_op jit(solution)/shard_map/ppermute | solution.py:192
  170.8 0.5 collective-permute-start.23
  171.3 0.3 copy-done.6
  171.7 0.5 collective-permute-start.24
  172.2 0.7 pad_add_fusion.where_ref
  172.8 0.3 collective-permute-done.22.refs_17_
  173.2 0.8 collective-permute-done.23.refs_18_
  174.0 0.8 collective-permute-done.24.refs_19_
  174.9 6.7 %project1.1 = bf16[128,3072]{1,0:T(8,128)(2,1)} custom-call(s32[2]{0:T(128)} %pad_add_fusion.where_ref, bf16[2,128,384]{2,1,0:T(8,128)(2,1)} %get-tuple-element.25.refs_0_, bf16[2,128,384]{2,1,0:T(8,128)(2,1)} %copy-done.8, bf16[2,128,384]{2,1,0:T(8,128)(2,1)} %copy-done.9, bf16[2,128,384]{2,1,0:T(8,128)(2,1)} %copy-done.10, bf16[384,768]{1,0:T(8,128)(2,1)} %refs_4_.3, ...), custom_call_target="tpu_custom_call" | custom-call | tf_op jit(solution)/shard_map/project1/pallas_call | solution.py:211
  181.6 0.5 collective-permute-start.25
  182.0 6.9 %project0.1 = f32[128,3072]{1,0:T(8,128)} custom-call(s32[2]{0:T(128)} %pad_add_fusion.where_ref, bf16[2,128,384]{2,1,0:T(8,128)(2,1)} %get-tuple-element.25.refs_0_, bf16[2,128,384]{2,1,0:T(8,128)(2,1)} %copy-done.8, bf16[2,128,384]{2,1,0:T(8,128)(2,1)} %copy-done.9, bf16[2,128,384]{2,1,0:T(8,128)(2,1)} %copy-done.10, bf16[384,768]{1,0:T(8,128)(2,1)} %refs_4_.3, ...), custom_call_target="tpu_custom_call" | custom-call | tf_op jit(solution)/shard_map/project0/pallas_call | solution.py:211
  189.0 12.4 %collective-permute-done.25 = bf16[128,3072]{1,0:T(8,128)(2,1)S(1)} collective-permute-done((bf16[128,3072]{1,0:T(8,128)(2,1)}, bf16[128,3072]{1,0:T(8,128)(2,1)S(1)}, u32[]{:S(2)}, u32[]{:S(2)}) %collective-permute-start.25) | collective-permute-done | bytes 786464 | tf_op jit(solution)/shard_map/ppermute | solution.py:180
  201.3 2.4 %fusion = bf16[1,128,3072]{2,1,0:T(8,128)(2,1)} fusion(f32[128,3072]{1,0:T(8,128)} %project0.1, bf16[128,3072]{1,0:T(8,128)(2,1)S(1)} %collective-permute-done.25), kind=kLoop, calls=%fused_computation.1 | loop fusion | flops 1179648 | bytes 3145728 | tf_op jit(solution)/shard_map/broadcast_in_dim | solution.py:227
  (48 shorter events, 0.1 us)
Async XLA Ops:
  3.9 71.8 %copy-start = (bf16[384,768]{1,0:T(8,128)(2,1)S(1)}, bf16[384,768]{1,0:T(8,128)(2,1)}, u32[]{:S(2)}) copy-start(bf16[384,768]{1,0:T(8,128)(2,1)} %refs_4_.3) | copy-start | bytes 1769476
  3.9 13.3 %collective-permute-start = (bf16[3,128,384]{2,1,0:T(8,128)(2,1)}, bf16[3,128,384]{2,1,0:T(8,128)(2,1)S(1)}, u32[]{:S(2)}, u32[]{:S(2)}) collective-permute-start(bf16[3,128,384]{2,1,0:T(8,128)(2,1)} %get-tuple-element.18), channel_id=1, source_target_pairs={{0,4},{4,8},{8,12},{12,0},{16,20},{20,24},{24,28},{28,16},{1,5},{5... | collective-permute-start | bytes 884744 | tf_op jit(solution)/shard_map/ppermute | solution.py:180
  7.0 24.7 %collective-permute-start.1 = (bf16[3,128,384]{2,1,0:T(8,128)(2,1)}, bf16[3,128,384]{2,1,0:T(8,128)(2,1)S(1)}, u32[]{:S(2)}, u32[]{:S(2)}) collective-permute-start(bf16[3,128,384]{2,1,0:T(8,128)(2,1)} %get-tuple-element.19), channel_id=1, source_target_pairs={{0,8},{4,12},{8,0},{12,4},{16,24},{20,28},{24,16},{28,20},{1,9},{5... | collective-permute-start | bytes 884744 | tf_op jit(solution)/shard_map/ppermute | solution.py:180
  9.6 40.1 %collective-permute-start.2 = (bf16[3,128,384]{2,1,0:T(8,128)(2,1)}, bf16[3,128,384]{2,1,0:T(8,128)(2,1)S(1)}, u32[]{:S(2)}, u32[]{:S(2)}) collective-permute-start(bf16[3,128,384]{2,1,0:T(8,128)(2,1)} %get-tuple-element.20), channel_id=1, source_target_pairs={{0,12},{4,0},{8,4},{12,8},{16,28},{20,16},{24,20},{28,24},{1,13},{... | collective-permute-start | bytes 884744 | tf_op jit(solution)/shard_map/ppermute | solution.py:180
  10.9 38.8 %collective-permute-start.3 = (bf16[3,128,384]{2,1,0:T(8,128)(2,1)}, bf16[3,128,384]{2,1,0:T(8,128)(2,1)S(1)}, u32[]{:S(2)}, u32[]{:S(2)}) collective-permute-start(bf16[3,128,384]{2,1,0:T(8,128)(2,1)} %get-tuple-element.21), channel_id=1, source_target_pairs={{0,16},{4,20},{8,24},{12,28},{16,0},{20,4},{24,8},{28,12},{1,17},{... | collective-permute-start | bytes 884744 | tf_op jit(solution)/shard_map/ppermute | solution.py:180
  12.4 37.3 %collective-permute-start.4 = (bf16[3,128,384]{2,1,0:T(8,128)(2,1)}, bf16[3,128,384]{2,1,0:T(8,128)(2,1)S(1)}, u32[]{:S(2)}, u32[]{:S(2)}) collective-permute-start(bf16[3,128,384]{2,1,0:T(8,128)(2,1)} %get-tuple-element.22), channel_id=1, source_target_pairs={{0,20},{4,24},{8,28},{12,16},{16,4},{20,8},{24,12},{28,0},{1,21},{... | collective-permute-start | bytes 884744 | tf_op jit(solution)/shard_map/ppermute | solution.py:180
  17.2 39.7 %copy-start.11 = (bf16[3,128,384]{2,1,0:T(8,128)(2,1)}, bf16[3,128,384]{2,1,0:T(8,128)(2,1)S(1)}, u32[]{:S(2)}) copy-start(bf16[3,128,384]{2,1,0:T(8,128)(2,1)S(1)} %collective-permute-done.refs_1_) | copy-start | bytes 884740
  17.2 38.0 %collective-permute-start.5 = (bf16[3,128,384]{2,1,0:T(8,128)(2,1)}, bf16[3,128,384]{2,1,0:T(8,128)(2,1)S(1)}, u32[]{:S(2)}, u32[]{:S(2)}) collective-permute-start(bf16[3,128,384]{2,1,0:T(8,128)(2,1)} %get-tuple-element.23), channel_id=1, source_target_pairs={{0,24},{4,28},{8,16},{12,20},{16,8},{20,12},{24,0},{28,4},{1,25},{... | collective-permute-start | bytes 884744 | tf_op jit(solution)/shard_map/ppermute | solution.py:180
  31.7 25.2 %copy-start.12 = (bf16[3,128,384]{2,1,0:T(8,128)(2,1)}, bf16[3,128,384]{2,1,0:T(8,128)(2,1)S(1)}, u32[]{:S(2)}) copy-start(bf16[3,128,384]{2,1,0:T(8,128)(2,1)S(1)} %collective-permute-done.1.refs_2_) | copy-start | bytes 884740
  31.7 25.2 %collective-permute-start.6 = (bf16[3,128,384]{2,1,0:T(8,128)(2,1)}, bf16[3,128,384]{2,1,0:T(8,128)(2,1)S(1)}, u32[]{:S(2)}, u32[]{:S(2)}) collective-permute-start(bf16[3,128,384]{2,1,0:T(8,128)(2,1)} %get-tuple-element.24), channel_id=1, source_target_pairs={{0,28},{4,16},{8,20},{12,24},{16,12},{20,0},{24,4},{28,8},{1,29},{... | collective-permute-start | bytes 884744 | tf_op jit(solution)/shard_map/ppermute | solution.py:180
  49.7 7.2 %copy-start.13 = (bf16[3,128,384]{2,1,0:T(8,128)(2,1)}, bf16[3,128,384]{2,1,0:T(8,128)(2,1)S(1)}, u32[]{:S(2)}) copy-start(bf16[3,128,384]{2,1,0:T(8,128)(2,1)S(1)} %collective-permute-done.2.refs_3_) | copy-start | bytes 884740
  49.7 7.2 %copy-start.14 = (bf16[3,128,384]{2,1,0:T(8,128)(2,1)}, bf16[3,128,384]{2,1,0:T(8,128)(2,1)S(1)}, u32[]{:S(2)}) copy-start(bf16[3,128,384]{2,1,0:T(8,128)(2,1)S(1)} %collective-permute-done.3.refs_4_) | copy-start | bytes 884740
  49.7 7.2 %copy-start.15 = (bf16[3,128,384]{2,1,0:T(8,128)(2,1)}, bf16[3,128,384]{2,1,0:T(8,128)(2,1)S(1)}, u32[]{:S(2)}) copy-start(bf16[3,128,384]{2,1,0:T(8,128)(2,1)S(1)} %collective-permute-done.4.refs_5_) | copy-start | bytes 884740
  55.2 1.7 copy-start.16
  56.9 0.7 copy-start.17
  68.8 11.9 %collective-permute-start.7 = (bf16[2,128,384]{2,1,0:T(8,128)(2,1)}, bf16[2,128,384]{2,1,0:T(8,128)(2,1)S(1)}, u32[]{:S(2)}, u32[]{:S(2)}) collective-permute-start(bf16[2,128,384]{2,1,0:T(8,128)(2,1)} %get-tuple-element.26), channel_id=1, source_target_pairs={{0,12},{4,0},{8,4},{12,8},{16,28},{20,16},{24,20},{28,24},{1,13},{... | collective-permute-start | bytes 589832 | tf_op jit(solution)/shard_map/ppermute | solution.py:180
  75.1 44.3 %collective-permute-start.8 = (bf16[2,128,384]{2,1,0:T(8,128)(2,1)}, bf16[2,128,384]{2,1,0:T(8,128)(2,1)S(1)}, u32[]{:S(2)}, u32[]{:S(2)}) collective-permute-start(bf16[2,128,384]{2,1,0:T(8,128)(2,1)} %get-tuple-element.27), channel_id=1, source_target_pairs={{0,8},{4,12},{8,0},{12,4},{16,24},{20,28},{24,16},{28,20},{1,9},{5... | collective-permute-start | bytes 589832 | tf_op jit(solution)/shard_map/ppermute | solution.py:180
  75.4 45.5 %collective-permute-start.9 = (bf16[2,128,384]{2,1,0:T(8,128)(2,1)}, bf16[2,128,384]{2,1,0:T(8,128)(2,1)S(1)}, u32[]{:S(2)}, u32[]{:S(2)}) collective-permute-start(bf16[2,128,384]{2,1,0:T(8,128)(2,1)} %get-tuple-element.28), channel_id=1, source_target_pairs={{0,4},{4,8},{8,12},{12,0},{16,20},{20,24},{24,28},{28,16},{1,5},{5... | collective-permute-start | bytes 589832 | tf_op jit(solution)/shard_map/ppermute | solution.py:180
  75.7 45.2 %collective-permute-start.10 = (bf16[384,768]{1,0:T(8,128)(2,1)S(1)}, bf16[384,768]{1,0:T(8,128)(2,1)S(1)}, u32[]{:S(2)}, u32[]{:S(2)}) collective-permute-start(bf16[384,768]{1,0:T(8,128)(2,1)S(1)} %copy-done), channel_id=1, source_target_pairs={{0,4},{4,8},{8,12},{12,0},{16,20},{20,24},{24,28},{28,16},{1,5},{5... | collective-permute-start | bytes 1769480 | tf_op jit(solution)/shard_map/ppermute | solution.py:180
  78.6 53.4 %collective-permute-start.11 = (bf16[384,768]{1,0:T(8,128)(2,1)S(1)}, bf16[384,768]{1,0:T(8,128)(2,1)S(1)}, u32[]{:S(2)}, u32[]{:S(2)}) collective-permute-start(bf16[384,768]{1,0:T(8,128)(2,1)S(1)} %copy-done), channel_id=1, source_target_pairs={{0,8},{4,12},{8,0},{12,4},{16,24},{20,28},{24,16},{28,20},{1,9},{5... | collective-permute-start | bytes 1769480 | tf_op jit(solution)/shard_map/ppermute | solution.py:180
  80.7 62.9 %copy-start.8 = (bf16[2,128,384]{2,1,0:T(8,128)(2,1)}, bf16[2,128,384]{2,1,0:T(8,128)(2,1)S(1)}, u32[]{:S(2)}) copy-start(bf16[2,128,384]{2,1,0:T(8,128)(2,1)S(1)} %collective-permute-done.7.refs_1_) | copy-start | bytes 589828
  80.7 61.5 %collective-permute-start.12 = (bf16[384,768]{1,0:T(8,128)(2,1)S(1)}, bf16[384,768]{1,0:T(8,128)(2,1)S(1)}, u32[]{:S(2)}, u32[]{:S(2)}) collective-permute-start(bf16[384,768]{1,0:T(8,128)(2,1)S(1)} %copy-done), channel_id=1, source_target_pairs={{0,12},{4,0},{8,4},{12,8},{16,28},{20,16},{24,20},{28,24},{1,13},{... | collective-permute-start | bytes 1769480 | tf_op jit(solution)/shard_map/ppermute | solution.py:180
  119.4 24.3 %copy-start.9 = (bf16[2,128,384]{2,1,0:T(8,128)(2,1)}, bf16[2,128,384]{2,1,0:T(8,128)(2,1)S(1)}, u32[]{:S(2)}) copy-start(bf16[2,128,384]{2,1,0:T(8,128)(2,1)S(1)} %collective-permute-done.8.refs_2_) | copy-start | bytes 589828
  119.4 24.3 %collective-permute-start.17 = (bf16[384,768]{1,0:T(8,128)(2,1)S(1)}, bf16[384,768]{1,0:T(8,128)(2,1)S(1)}, u32[]{:S(2)}, u32[]{:S(2)}) collective-permute-start(bf16[384,768]{1,0:T(8,128)(2,1)S(1)} %copy-done), channel_id=1, source_target_pairs={{0,2},{1,3},{2,0},{3,1},{4,6},{5,7},{6,4},{7,5},{8,10},{9,11},{10,... | collective-permute-start | bytes 1769480 | tf_op jit(solution)/shard_map/ppermute | solution.py:192
  120.9 22.8 %copy-start.10 = (bf16[2,128,384]{2,1,0:T(8,128)(2,1)}, bf16[2,128,384]{2,1,0:T(8,128)(2,1)S(1)}, u32[]{:S(2)}) copy-start(bf16[2,128,384]{2,1,0:T(8,128)(2,1)S(1)} %collective-permute-done.9.refs_3_) | copy-start | bytes 589828
  120.9 22.9 %collective-permute-start.13 = (bf16[384,768]{1,0:T(8,128)(2,1)S(1)}, bf16[384,768]{1,0:T(8,128)(2,1)S(1)}, u32[]{:S(2)}, u32[]{:S(2)}) collective-permute-start(bf16[384,768]{1,0:T(8,128)(2,1)S(1)} %copy-done), channel_id=1, source_target_pairs={{0,1},{1,0},{2,3},{3,2},{4,5},{5,4},{6,7},{7,6},{8,9},{9,8},{10,11... | collective-permute-start | bytes 1769480 | tf_op jit(solution)/shard_map/ppermute | solution.py:192
  120.9 54.0 %copy-start.1 = (bf16[384,768]{1,0:T(8,128)(2,1)}, bf16[384,768]{1,0:T(8,128)(2,1)S(1)}, u32[]{:S(2)}) copy-start(bf16[384,768]{1,0:T(8,128)(2,1)S(1)} %collective-permute-done.10.refs_5_) | copy-start | bytes 1769476
  120.9 27.4 %collective-permute-start.18 = (bf16[384,768]{1,0:T(8,128)(2,1)S(1)}, bf16[384,768]{1,0:T(8,128)(2,1)}, u32[]{:S(2)}, u32[]{:S(2)}) collective-permute-start(bf16[384,768]{1,0:T(8,128)(2,1)S(1)} %collective-permute-done.10.refs_5_), channel_id=1, source_target_pairs={{0,2},{1,3},{2,0},{3,1},{4,6},{5,7},{6,4},{7,5},{8,10},{9,11},{10,... | collective-permute-start | bytes 1769480 | tf_op jit(solution)/shard_map/ppermute | solution.py:192
  131.9 42.9 %copy-start.2 = (bf16[384,768]{1,0:T(8,128)(2,1)}, bf16[384,768]{1,0:T(8,128)(2,1)S(1)}, u32[]{:S(2)}) copy-start(bf16[384,768]{1,0:T(8,128)(2,1)S(1)} %collective-permute-done.11.refs_6_) | copy-start | bytes 1769476
  131.9 29.0 %collective-permute-start.19 = (bf16[384,768]{1,0:T(8,128)(2,1)S(1)}, bf16[384,768]{1,0:T(8,128)(2,1)}, u32[]{:S(2)}, u32[]{:S(2)}) collective-permute-start(bf16[384,768]{1,0:T(8,128)(2,1)S(1)} %collective-permute-done.11.refs_6_), channel_id=1, source_target_pairs={{0,2},{1,3},{2,0},{3,1},{4,6},{5,7},{6,4},{7,5},{8,10},{9,11},{10,... | collective-permute-start | bytes 1769480 | tf_op jit(solution)/shard_map/ppermute | solution.py:192
  142.2 32.6 %copy-start.3 = (bf16[384,768]{1,0:T(8,128)(2,1)}, bf16[384,768]{1,0:T(8,128)(2,1)S(1)}, u32[]{:S(2)}) copy-start(bf16[384,768]{1,0:T(8,128)(2,1)S(1)} %collective-permute-done.12.refs_7_) | copy-start | bytes 1769476
  142.2 28.6 %collective-permute-start.20 = (bf16[384,768]{1,0:T(8,128)(2,1)S(1)}, bf16[384,768]{1,0:T(8,128)(2,1)}, u32[]{:S(2)}, u32[]{:S(2)}) collective-permute-start(bf16[384,768]{1,0:T(8,128)(2,1)S(1)} %collective-permute-done.12.refs_7_), channel_id=1, source_target_pairs={{0,2},{1,3},{2,0},{3,1},{4,6},{5,7},{6,4},{7,5},{8,10},{9,11},{10,... | collective-permute-start | bytes 1769480 | tf_op jit(solution)/shard_map/ppermute | solution.py:192
  143.7 31.2 %copy-start.4 = (bf16[384,768]{1,0:T(8,128)(2,1)}, bf16[384,768]{1,0:T(8,128)(2,1)S(1)}, u32[]{:S(2)}) copy-start(bf16[384,768]{1,0:T(8,128)(2,1)S(1)} %collective-permute-done.17.refs_12_) | copy-start | bytes 1769476
  143.7 27.1 %collective-permute-start.14 = (bf16[384,768]{1,0:T(8,128)(2,1)S(1)}, bf16[384,768]{1,0:T(8,128)(2,1)S(1)}, u32[]{:S(2)}, u32[]{:S(2)}) collective-permute-start(bf16[384,768]{1,0:T(8,128)(2,1)S(1)} %collective-permute-done.10.refs_5_), channel_id=1, source_target_pairs={{0,1},{1,0},{2,3},{3,2},{4,5},{5,4},{6,7},{7,6},{8,9},{9,8},{10,11... | collective-permute-start | bytes 1769480 | tf_op jit(solution)/shard_map/ppermute | solution.py:192
  143.8 31.1 %copy-start.5 = (bf16[384,768]{1,0:T(8,128)(2,1)}, bf16[384,768]{1,0:T(8,128)(2,1)S(1)}, u32[]{:S(2)}) copy-start(bf16[384,768]{1,0:T(8,128)(2,1)S(1)} %collective-permute-done.13.refs_8_) | copy-start | bytes 1769476
  143.8 27.6 %collective-permute-start.15 = (bf16[384,768]{1,0:T(8,128)(2,1)S(1)}, bf16[384,768]{1,0:T(8,128)(2,1)S(1)}, u32[]{:S(2)}, u32[]{:S(2)}) collective-permute-start(bf16[384,768]{1,0:T(8,128)(2,1)S(1)} %collective-permute-done.11.refs_6_), channel_id=1, source_target_pairs={{0,1},{1,0},{2,3},{3,2},{4,5},{5,4},{6,7},{7,6},{8,9},{9,8},{10,11... | collective-permute-start | bytes 1769480 | tf_op jit(solution)/shard_map/ppermute | solution.py:192
  148.3 24.5 %collective-permute-start.16 = (bf16[384,768]{1,0:T(8,128)(2,1)S(1)}, bf16[384,768]{1,0:T(8,128)(2,1)}, u32[]{:S(2)}, u32[]{:S(2)}) collective-permute-start(bf16[384,768]{1,0:T(8,128)(2,1)S(1)} %collective-permute-done.12.refs_7_), channel_id=1, source_target_pairs={{0,1},{1,0},{2,3},{3,2},{4,5},{5,4},{6,7},{7,6},{8,9},{9,8},{10,11... | collective-permute-start | bytes 1769480 | tf_op jit(solution)/shard_map/ppermute | solution.py:192
  160.9 11.9 %collective-permute-start.21 = (bf16[384,768]{1,0:T(8,128)(2,1)S(1)}, bf16[384,768]{1,0:T(8,128)(2,1)}, u32[]{:S(2)}, u32[]{:S(2)}) collective-permute-start(bf16[384,768]{1,0:T(8,128)(2,1)S(1)} %collective-permute-done.17.refs_12_), channel_id=1, source_target_pairs={{0,1},{1,0},{2,3},{3,2},{4,5},{5,4},{6,7},{7,6},{8,9},{9,8},{10,11... | collective-permute-start | bytes 1769480 | tf_op jit(solution)/shard_map/ppermute | solution.py:192
  170.8 2.3 %collective-permute-start.22 = (bf16[384,768]{1,0:T(8,128)(2,1)}, bf16[384,768]{1,0:T(8,128)(2,1)}, u32[]{:S(2)}, u32[]{:S(2)}) collective-permute-start(bf16[384,768]{1,0:T(8,128)(2,1)} %collective-permute-done.18.refs_13_), channel_id=1, source_target_pairs={{0,1},{1,0},{2,3},{3,2},{4,5},{5,4},{6,7},{7,6},{8,9},{9,8},{10,11... | collective-permute-start | bytes 1769480 | tf_op jit(solution)/shard_map/ppermute | solution.py:192
  170.8 0.8 copy-start.6
  170.8 3.2 %collective-permute-start.23 = (bf16[384,768]{1,0:T(8,128)(2,1)}, bf16[384,768]{1,0:T(8,128)(2,1)}, u32[]{:S(2)}, u32[]{:S(2)}) collective-permute-start(bf16[384,768]{1,0:T(8,128)(2,1)} %collective-permute-done.19.refs_14_), channel_id=1, source_target_pairs={{0,1},{1,0},{2,3},{3,2},{4,5},{5,4},{6,7},{7,6},{8,9},{9,8},{10,11... | collective-permute-start | bytes 1769480 | tf_op jit(solution)/shard_map/ppermute | solution.py:192
  171.7 3.2 %copy-start.7 = (bf16[384,768]{1,0:T(8,128)(2,1)}, bf16[384,768]{1,0:T(8,128)(2,1)S(1)}, u32[]{:S(2)}) copy-start(bf16[384,768]{1,0:T(8,128)(2,1)S(1)} %collective-permute-done.15.refs_10_) | copy-start | bytes 1769476
  171.7 3.2 %collective-permute-start.24 = (bf16[384,768]{1,0:T(8,128)(2,1)}, bf16[384,768]{1,0:T(8,128)(2,1)}, u32[]{:S(2)}, u32[]{:S(2)}) collective-permute-start(bf16[384,768]{1,0:T(8,128)(2,1)} %collective-permute-done.20.refs_15_), channel_id=1, source_target_pairs={{0,1},{1,0},{2,3},{3,2},{4,5},{5,4},{6,7},{7,6},{8,9},{9,8},{10,11... | collective-permute-start | bytes 1769480 | tf_op jit(solution)/shard_map/ppermute | solution.py:192
  181.6 19.8 %collective-permute-start.25 = (bf16[128,3072]{1,0:T(8,128)(2,1)}, bf16[128,3072]{1,0:T(8,128)(2,1)S(1)}, u32[]{:S(2)}, u32[]{:S(2)}) collective-permute-start(bf16[128,3072]{1,0:T(8,128)(2,1)} %project1.1), channel_id=1, source_target_pairs={{0,16},{4,20},{8,24},{12,28},{16,0},{20,4},{24,8},{28,12},{1,17},{... | collective-permute-start | bytes 2359304 | tf_op jit(solution)/shard_map/ppermute | solution.py:180

commit v2 on v1

--- a/solution.py
+++ b/solution.py
@@ -7,6 +7,7 @@
 from jax.experimental import pallas as pl
 from jax.experimental.pallas import tpu as pltpu
 from jax.sharding import PartitionSpec as P
+
 
 HS = 128
 LOG2E = math.log2(math.e)
@@ -87,13 +88,21 @@
     return summed.astype(jnp.bfloat16)[None]
 
 
-def pack_kernel(dest_ref, q_ref, k_ref, v_ref, *out_refs):
-    width = out_refs[0].shape[-1]
-    for j, out_ref in enumerate(out_refs):
-        cols = pl.ds(pl.multiple_of(dest_ref[j] * width, HS), width)
-        out_ref[0] = q_ref[:, cols]
-        out_ref[1] = k_ref[:, cols]
-        out_ref[2] = v_ref[:, cols]
+def head_chunks(width):
+    heads = width // HS
+    cuts = [0, heads - heads // 2 if heads > 2 else 1, heads] if heads > 1 else [0, heads]
+    return [(lo * HS, hi * HS) for lo, hi in zip(cuts, cuts[1:])]
+
+
+def pack_kernel(dest_ref, q_ref, k_ref, v_ref, *out_refs, groups):
+    width = q_ref.shape[1] // groups
+    for c, (lo, hi) in enumerate(head_chunks(width)):
+        for j in range(groups):
+            out_ref = out_refs[c * groups + j]
+            cols = pl.ds(pl.multiple_of(dest_ref[j] * width + lo, HS), hi - lo)
+            out_ref[0] = q_ref[:, cols]
+            out_ref[1] = k_ref[:, cols]
+            out_ref[2] = v_ref[:, cols]
 
 
 def attend_kernel(pos_ref, *refs, n_seq, n_tensor):
@@ -127,12 +136,13 @@
 
 
 def project_kernel(where_ref, *refs, row_set, n_tensor, n_bucket):
-    pieces, weights = refs[:n_tensor], refs[n_tensor : n_tensor + n_bucket * n_tensor]
-    out_ref, o_scr = refs[n_tensor + n_bucket * n_tensor :]
+    *ins, out_ref, o_scr = refs
+    pieces, weights = ins[: -n_bucket * n_tensor], ins[-n_bucket * n_tensor :]
     width = weights[0].shape[1]
     z, b = where_ref[0], where_ref[1]
-    for dz in range(n_tensor):
-        o_scr[lax.rem(z + dz, n_tensor)] = pieces[dz][row_set]
+    for c, (lo, hi) in enumerate(head_chunks(o_scr.shape[-1])):
+        for dz in range(n_tensor):
+            o_scr[lax.rem(z + dz, n_tensor), :, lo:hi] = pieces[c * n_tensor + dz][row_set]
     for dz in range(n_tensor):
         acc = None
         for m in range(n_bucket):
@@ -141,11 +151,11 @@
                 preferred_element_type=jnp.float32,
             )
             acc = part if acc is None else acc + part
-        place = pl.multiple_of(lax.rem(z - dz + n_tensor, n_tensor) * width, HS)
+        place = pl.multiple_of(jnp.bitwise_xor(z, dz) * width, HS)
         out_ref[:, pl.ds(place, width)] = acc.astype(out_ref.dtype)
 
 
-def vmem_call(kernel, n_in, out_shape, scratch=(), name=None):
+def vmem_call(kernel, n_in, out_shape, scratch=()):
     vmem = pl.BlockSpec(memory_space=pltpu.VMEM)
     return pl.pallas_call(
         kernel,
@@ -153,11 +163,14 @@
         out_specs=[vmem] * len(out_shape),
         out_shape=out_shape,
         scratch_shapes=scratch,
-        name=name,
-    )
-
-
-def head_shards(queries, keys, values, lengths, out_weight):
+    )
+
+
+def head_shards(*args):
+    return head_step(*args)
+
+
+def head_step(queries, keys, values, lengths, out_weight):
     n_seq, n_tensor, n_bucket = (lax.axis_size(a) for a in ("seq", "tensor", "bucket"))
     s, z, b = (lax.axis_index(a).astype(jnp.int32) for a in ("seq", "tensor", "bucket"))
     groups = n_seq * n_tensor
@@ -167,8 +180,11 @@
     shifts = [(ds, dz) for ds in range(n_seq) for dz in range(n_tensor)]
 
     dest = jnp.stack([(s + ds) % n_seq * n_tensor + (z + dz) % n_tensor for ds, dz in shifts])
+    chunks = head_chunks(width)
     packed = vmem_call(
-        pack_kernel, 3, [jax.ShapeDtypeStruct((3, rows, width), bf16)] * groups, name="pack"
+        functools.partial(pack_kernel, groups=groups),
+        3,
+        [jax.ShapeDtypeStruct((3, rows, hi - lo), bf16) for lo, hi in chunks for _ in range(groups)],
     )(dest, queries[0], keys[0], values[0])
 
     def shifted(x, ds, dz):
@@ -179,18 +195,28 @@
         ]
         return lax.ppermute(x, ("seq", "tensor"), perm)
 
-    blocks = [packed[0]] + [shifted(packed[j], *shifts[j]) for j in range(1, groups)]
-
-    weights = [out_weight]
-    for dz in range(1, n_tensor):
-        weights.append(shifted(out_weight, 0, dz))
+    blocks = [
+        [packed[c * groups]]
+        + [shifted(packed[c * groups + j], *shifts[j]) for j in range(1, groups)]
+        for c in range(len(chunks))
+    ]
+
+    weights = {0: out_weight}
+    bit = n_tensor // 2
+    while bit:
+        swap = [(i, i ^ bit) for i in range(n_tensor)]
+        for e in list(weights):
+            weights[e ^ bit] = lax.ppermute(weights[e], "tensor", swap)
+        bit //= 2
+    weights = [weights[e] for e in range(n_tensor)]
     bit = n_bucket // 2
     held = {0: weights}
     while bit:
         swap = [(i, i ^ bit) for i in range(n_bucket)]
-        held.update(
-            {m ^ bit: [lax.ppermute(w, "bucket", swap) for w in held[m]] for m in list(held)}
-        )
+        for m in list(held):
+            held[m ^ bit] = []
+            for w in held[m]:
+                held[m ^ bit].append(lax.ppermute(w, "bucket", swap))
         bit //= 2
     flat_weights = [w for m in range(n_bucket) for w in held[m]]
 
@@ -198,29 +224,28 @@
         [((s - ds) % n_seq * n_tensor + (z - dz) % n_tensor) * rows for ds, dz in shifts]
         + [lengths[0]]
     )
-    mixed = vmem_call(
-        functools.partial(attend_kernel, n_seq=n_seq, n_tensor=n_tensor),
-        groups,
-        [jax.ShapeDtypeStruct((n_seq, rows, width), bf16)] * n_tensor,
-        [pltpu.VMEM((width // HS, groups * rows, HS), bf16)] * 2,
-        name="attend",
-    )(pos, *blocks)
-    pieces = [mixed[0]] + [shifted(mixed[dz], 0, -dz) for dz in range(1, n_tensor)]
+    pieces = []
+    for c, (lo, hi) in enumerate(chunks):
+        mixed = vmem_call(
+            functools.partial(attend_kernel, n_seq=n_seq, n_tensor=n_tensor),
+            groups,
+            [jax.ShapeDtypeStruct((n_seq, rows, hi - lo), bf16)] * n_tensor,
+            [pltpu.VMEM(((hi - lo) // HS, groups * rows, HS), bf16)] * 2,
+        )(pos, *blocks[c])
+        pieces.append(mixed[0])
+        pieces += [shifted(mixed[dz], 0, -dz) for dz in range(1, n_tensor)]
 
     def project(row_set, dtype):
         return vmem_call(
             functools.partial(
                 project_kernel, row_set=row_set, n_tensor=n_tensor, n_bucket=n_bucket
             ),
-            n_tensor + n_tensor * n_bucket,
+            len(pieces) + n_tensor * n_bucket,
             [jax.ShapeDtypeStruct((rows, model), dtype)],
             [pltpu.VMEM((n_tensor, rows, width), bf16)],
-            name=f"project{row_set}",
         )(jnp.stack([z, b]), *pieces, *flat_weights)[0]
 
-    received = [
-        shifted(project(ds, bf16), -ds, 0) for ds in range(1, n_seq)
-    ]
+    received = [shifted(project(ds, bf16), -ds, 0) for ds in range(1, n_seq)]
     summed = project(0, f32)
     for other in received:
         summed = summed + other.astype(f32)
@@ -235,11 +260,13 @@
         by_head = (
             heads % (n_seq * n_tensor) == 0
             and n_tensor == n_bucket
+            and 1 < n_bucket
             and n_bucket & (n_bucket - 1) == 0
         )
-        return jax.shard_map(
+        step = jax.shard_map(
             head_shards if by_head else shards,
             mesh=mesh, in_specs=IN_SPECS, out_specs=OUT_SPECS, check_vma=False,
-        )(queries, keys, values, lengths, out_weight)
+        )
+        return step(queries, keys, values, lengths, out_weight)
 
     return run

time: 204 us -> 215 us (1.054)
  waiting for transfers between devices: 107 us -> 121 us
  starting transfers between devices: 62.6 us -> 56.6 us
    ppermute x14 -> x21, waiting for transfers between devices: 78.3 us -> 88.7 us  [shifted(): return lax.ppermute(x, ('seq', 'tensor'), perm)]
    ppermute x14 -> x21, starting transfers between devices: 56 us -> 46 us  [shifted(): return lax.ppermute(x, ('seq', 'tensor'), perm)]
    ppermute x12 -> x15, starting transfers between devices: 6.63 us -> 10.6 us  [the longest x12 5.92 us: head_step(): held[m ^ bit].append(lax.ppermute(w, 'bucket', swap))]
    ppermute x12 -> x15, waiting for transfers between devices: 28.6 us -> 32.5 us  [the longest x12 32.5 us: head_step(): held[m ^ bit].append(lax.ppermute(w, 'bucket', swap))]
    pallas_call x2 -> x3, Pallas kernels: 14.4 us -> 16.3 us  [the longest x2 12.9 us: head_step(): vmem_call(functools.partial(attend_kernel, n_seq=n_seq, n_tensor=n_tensor...]
  transfers between devices with their start and end apart: 26 -> 36, of which waited for: 14 -> 15; matrix products, arithmetic and copies ran while one was open for 1% -> 1% of each run, Pallas kernels for 3% -> 9%
where the time goes in v2:
time: 215 us
  waiting for transfers between devices  121 us (56%)
  starting transfers between devices  56.6 us (26%)
  Pallas kernels  30 us (14%)
  local copies, waits for them, and re-layouts  3.09 us (1%)
  other arithmetic  3.09 us (1%)
    ppermute x21, waiting for transfers between devices, shifted(): return lax.ppermute(x, ('seq', 'tensor'), perm)  88.7 us
    ppermute x21, starting transfers between devices, shifted(): return lax.ppermute(x, ('seq', 'tensor'), perm)  46 us
    ppermute x12, waiting for transfers between devices, head_step(): held[m ^ bit].append(lax.ppermute(w, 'bucket', swap))  32.5 us
    pallas_call x2, Pallas kernels, project(): vmem_call(functools.partial(project_kernel, row_set=row_set, n_tensor=n_t...  13.7 us
    pallas_call x2, Pallas kernels, head_step(): vmem_call(functools.partial(attend_kernel, n_seq=n_seq, n_tensor=n_tensor...  12.9 us
    ppermute x12, starting transfers between devices, head_step(): held[m ^ bit].append(lax.ppermute(w, 'bucket', swap))  5.92 us
    ppermute x3, starting transfers between devices, head_step(): weights[e ^ bit] = lax.ppermute(weights[e], 'tensor', swap)  4.71 us
  transfers between devices with their start and end apart: 36, of which 15 were waited for; matrix products, arithmetic and copies ran while one was open for 1% of the time, Pallas kernels for 9%

profile of v2, /device:TPU:0, one launch (start us, length us, event | category | flops | bytes accessed | tf_op | source)
XLA Modules:
  0.0 214.8 jit_solution(11287664016348423911)
XLA Ops:
  0.0 0.6 stack.86.dest_ref
  0.6 3.4 %shard_map.55 = (bf16[3,128,256]{2,1,0:T(8,128)(2,1)}, bf16[3,128,256]{2,1,0:T(8,128)(2,1)}, bf16[3,128,256]{2,1,0:T(8,128)(2,1)}, bf16[3,128,256]{2,1,0:T(8,128...) custom-call(s32[8]{0:T(128)} %stack.86.dest_ref, ...), custom_call_target="tpu_custom_call" | custom-call | tf_op jit(solution)/shard_map/pallas_call | solution.py:184
  4.0 3.1 %collective-permute-start.10 = (bf16[3,128,128]{2,1,0:T(8,128)(2,1)}, bf16[3,128,128]{2,1,0:T(8,128)(2,1)S(1)}, u32[]{:S(2)}, u32[]{:S(2)}) collective-permute-start(bf16[3,128,128]{2,1,0:T(8,128)(2,1)} %get-tuple-element.42), channel_id=1, source_target_pairs={{0,4},{4,8},{8,12},{12,0},{16,20},{20,24},{24,28},{28,16},{1,5},{5... | collective-permute-start | bytes 294920 | tf_op jit(solution)/shard_map/ppermute | solution.py:196
  7.1 2.6 %collective-permute-start.21 = (bf16[384,768]{1,0:T(8,128)(2,1)S(1)}, bf16[384,768]{1,0:T(8,128)(2,1)S(1)}, u32[]{:S(2)}, u32[]{:S(2)}) collective-permute-start(bf16[384,768]{1,0:T(8,128)(2,1)S(1)} %copy-done), channel_id=1, source_target_pairs={{0,8},{4,12},{8,0},{12,4},{1,9},{5,13},{9,1},{13,5},{2,10},{6,14},... | collective-permute-start | bytes 1769480 | tf_op jit(solution)/shard_map/ppermute | solution.py:209
  10.0 2.1 collective-permute-start.12
  12.1 1.6 collective-permute-start.13
  13.7 15.5 %collective-permute-start.14 = (bf16[3,128,128]{2,1,0:T(8,128)(2,1)}, bf16[3,128,128]{2,1,0:T(8,128)(2,1)S(1)}, u32[]{:S(2)}, u32[]{:S(2)}) collective-permute-start(bf16[3,128,128]{2,1,0:T(8,128)(2,1)} %get-tuple-element.46), channel_id=1, source_target_pairs={{0,20},{4,24},{8,28},{12,16},{16,4},{20,8},{24,12},{28,0},{1,21},{... | collective-permute-start | bytes 294920 | tf_op jit(solution)/shard_map/ppermute | solution.py:196
  29.3 14.5 %collective-permute-done.11.refs_2_ = bf16[3,128,128]{2,1,0:T(8,128)(2,1)S(1)} collective-permute-done((bf16[3,128,128]{2,1,0:T(8,128)(2,1)}, bf16[3,128,128]{2,1,0:T(8,128)(2,1)S(1)}, u32[]{:S(2)}, u32[]{:S(2)}) %collective-permute-start.11) | collective-permute-done | bytes 98336 | tf_op jit(solution)/shard_map/ppermute | solution.py:196
  43.8 0.6 collective-permute-start.15
  44.4 3.0 %collective-permute-start.16 = (bf16[3,128,128]{2,1,0:T(8,128)(2,1)}, bf16[3,128,128]{2,1,0:T(8,128)(2,1)S(1)}, u32[]{:S(2)}, u32[]{:S(2)}) collective-permute-start(bf16[3,128,128]{2,1,0:T(8,128)(2,1)} %get-tuple-element.48), channel_id=1, source_target_pairs={{0,28},{4,16},{8,20},{12,24},{16,12},{20,0},{24,4},{28,8},{1,29},{... | collective-permute-start | bytes 294920 | tf_op jit(solution)/shard_map/ppermute | solution.py:196
  47.4 0.6 collective-permute-start
  48.0 1.9 collective-permute-start.1
  50.6 0.6 stack.77.pos_ref
  51.2 2.3 %collective-permute-done.15.refs_6_ = bf16[3,128,128]{2,1,0:T(8,128)(2,1)S(1)} collective-permute-done((bf16[3,128,128]{2,1,0:T(8,128)(2,1)}, bf16[3,128,128]{2,1,0:T(8,128)(2,1)S(1)}, u32[]{:S(2)}, u32[]{:S(2)}) %collective-permute-start.15) | collective-permute-done | bytes 98336 | tf_op jit(solution)/shard_map/ppermute | solution.py:196
  53.5 2.4 %collective-permute-done.16.refs_7_ = bf16[3,128,128]{2,1,0:T(8,128)(2,1)S(1)} collective-permute-done((bf16[3,128,128]{2,1,0:T(8,128)(2,1)}, bf16[3,128,128]{2,1,0:T(8,128)(2,1)S(1)}, u32[]{:S(2)}, u32[]{:S(2)}) %collective-permute-start.16) | collective-permute-done | bytes 98336 | tf_op jit(solution)/shard_map/ppermute | solution.py:196
  55.9 0.6 copy-done.27
  56.5 4.8 %shard_map.57 = (bf16[2,128,128]{2,1,0:T(8,128)(2,1)}, bf16[2,128,128]{2,1,0:T(8,128)(2,1)}, bf16[2,128,128]{2,1,0:T(8,128)(2,1)}, bf16[2,128,128]{2,1,0:T(8,128)(2,1)}) custom-call(s32[9]{0:T(128)} %stack.77.pos_ref, bf16[3,128,128]{2,1,0:T(8,128)(2,1)} %get-tuple-element.41.refs_0_, bf16[3,128,128]{2,1,0:T(8,128)(2,1)} %copy-done.21, ...), custom_call_target="tpu_custom_call" | custom-call | tf_op jit(solution)/shard_map/pallas_call | solution.py:229
  61.5 7.7 %collective-permute-start.2 = (bf16[3,128,256]{2,1,0:T(8,128)(2,1)}, bf16[3,128,256]{2,1,0:T(8,128)(2,1)S(1)}, u32[]{:S(2)}, u32[]{:S(2)}) collective-permute-start(bf16[3,128,256]{2,1,0:T(8,128)(2,1)} %get-tuple-element.32), channel_id=1, source_target_pairs={{0,12},{4,0},{8,4},{12,8},{16,28},{20,16},{24,20},{28,24},{1,13},{... | collective-permute-start | bytes 589832 | tf_op jit(solution)/shard_map/ppermute | solution.py:196
  69.1 2.7 %collective-permute-done.17.refs_5_ = bf16[2,128,128]{2,1,0:T(8,128)(2,1)S(1)} collective-permute-done((bf16[2,128,128]{2,1,0:T(8,128)(2,1)}, bf16[2,128,128]{2,1,0:T(8,128)(2,1)S(1)}, u32[]{:S(2)}, u32[]{:S(2)}) %collective-permute-start.17) | collective-permute-done | bytes 65568 | tf_op jit(solution)/shard_map/ppermute | solution.py:196
  71.8 1.3 collective-permute-start.18
  73.1 4.1 %collective-permute-done.18.refs_6_ = bf16[2,128,128]{2,1,0:T(8,128)(2,1)S(1)} collective-permute-done((bf16[2,128,128]{2,1,0:T(8,128)(2,1)}, bf16[2,128,128]{2,1,0:T(8,128)(2,1)S(1)}, u32[]{:S(2)}, u32[]{:S(2)}) %collective-permute-start.18) | collective-permute-done | bytes 65568 | tf_op jit(solution)/shard_map/ppermute | solution.py:196
  77.2 1.9 collective-permute-start.3
  79.1 1.7 collective-permute-start.4
  80.9 1.3 collective-permute-start.5
  82.2 1.7 collective-permute-start.6
  84.0 11.8 %collective-permute-done.3.refs_4_ = bf16[3,128,256]{2,1,0:T(8,128)(2,1)S(1)} collective-permute-done((bf16[3,128,256]{2,1,0:T(8,128)(2,1)}, bf16[3,128,256]{2,1,0:T(8,128)(2,1)S(1)}, u32[]{:S(2)}, u32[]{:S(2)}) %collective-permute-start.3) | collective-permute-done | bytes 196640 | tf_op jit(solution)/shard_map/ppermute | solution.py:196
  95.7 1.5 collective-permute-start.27
  97.4 2.1 collective-permute-start.22
  99.6 0.6 copy-done.20
  100.1 8.1 %shard_map.56 = (bf16[2,128,256]{2,1,0:T(8,128)(2,1)}, bf16[2,128,256]{2,1,0:T(8,128)(2,1)}, bf16[2,128,256]{2,1,0:T(8,128)(2,1)}, bf16[2,128,256]{2,1,0:T(8,128)(2,1)}) custom-call(s32[9]{0:T(128)} %stack.77.pos_ref, bf16[3,128,256]{2,1,0:T(8,128)(2,1)} %get-tuple-element.29.refs_0_, bf16[3,128,256]{2,1,0:T(8,128)(2,1)} %copy-done.14, ...), custom_call_target="tpu_custom_call" | custom-call | tf_op jit(solution)/shard_map/pallas_call | solution.py:229
  108.2 19.1 %collective-permute-done.19.refs_7_ = bf16[2,128,128]{2,1,0:T(8,128)(2,1)} collective-permute-done((bf16[2,128,128]{2,1,0:T(8,128)(2,1)}, bf16[2,128,128]{2,1,0:T(8,128)(2,1)}, u32[]{:S(2)}, u32[]{:S(2)}) %collective-permute-start.19) | collective-permute-done | bytes 65568 | tf_op jit(solution)/shard_map/ppermute | solution.py:196
  127.3 5.2 %collective-permute-done.7.refs_1_ = bf16[2,128,256]{2,1,0:T(8,128)(2,1)S(1)} collective-permute-done((bf16[2,128,256]{2,1,0:T(8,128)(2,1)}, bf16[2,128,256]{2,1,0:T(8,128)(2,1)S(1)}, u32[]{:S(2)}, u32[]{:S(2)}) %collective-permute-start.7) | collective-permute-done | bytes 131104 | tf_op jit(solution)/shard_map/ppermute | solution.py:196
  132.5 8.7 %collective-permute-done.8.refs_2_ = bf16[2,128,256]{2,1,0:T(8,128)(2,1)S(1)} collective-permute-done((bf16[2,128,256]{2,1,0:T(8,128)(2,1)}, bf16[2,128,256]{2,1,0:T(8,128)(2,1)S(1)}, u32[]{:S(2)}, u32[]{:S(2)}) %collective-permute-start.8) | collective-permute-done | bytes 131104 | tf_op jit(solution)/shard_map/ppermute | solution.py:196
  141.2 0.6 copy-done.10
  141.9 6.3 %collective-permute-done.9.refs_3_ = bf16[2,128,256]{2,1,0:T(8,128)(2,1)S(1)} collective-permute-done((bf16[2,128,256]{2,1,0:T(8,128)(2,1)}, bf16[2,128,256]{2,1,0:T(8,128)(2,1)S(1)}, u32[]{:S(2)}, u32[]{:S(2)}) %collective-permute-start.9) | collective-permute-done | bytes 131104 | tf_op jit(solution)/shard_map/ppermute | solution.py:196
  148.2 1.7 collective-permute-start.29
  150.0 0.6 collective-permute-start.28
  150.7 1.4 collective-permute-start.30
  152.1 11.3 %collective-permute-done.29.refs_18_ = bf16[384,768]{1,0:T(8,128)(2,1)} collective-permute-done((bf16[384,768]{1,0:T(8,128)(2,1)S(1)}, bf16[384,768]{1,0:T(8,128)(2,1)}, u32[]{:S(2)}, u32[]{:S(2)}) %collective-permute-start.29) | collective-permute-done | bytes 589856 | tf_op jit(solution)/shard_map/ppermute | solution.py:219
  164.0 12.1 %collective-permute-done.28.refs_17_ = bf16[384,768]{1,0:T(8,128)(2,1)S(1)} collective-permute-done((bf16[384,768]{1,0:T(8,128)(2,1)S(1)}, bf16[384,768]{1,0:T(8,128)(2,1)S(1)}, u32[]{:S(2)}, u32[]{:S(2)}) %collective-permute-start.28) | collective-permute-done | bytes 589856 | tf_op jit(solution)/shard_map/ppermute | solution.py:219
  176.1 7.4 %collective-permute-done.30.refs_19_ = bf16[384,768]{1,0:T(8,128)(2,1)} collective-permute-done((bf16[384,768]{1,0:T(8,128)(2,1)S(1)}, bf16[384,768]{1,0:T(8,128)(2,1)}, u32[]{:S(2)}, u32[]{:S(2)}) %collective-permute-start.30) | collective-permute-done | bytes 589856 | tf_op jit(solution)/shard_map/ppermute | solution.py:219
  183.5 0.7 pad_add_fusion.where_ref
  184.2 1.7 collective-permute-done.34.refs_23_
  185.9 6.7 %shard_map.59 = bf16[128,3072]{1,0:T(8,128)(2,1)} custom-call(s32[2]{0:T(128)} %pad_add_fusion.where_ref, bf16[2,128,256]{2,1,0:T(8,128)(2,1)} %get-tuple-element.37.refs_0_, bf16[2,128,256]{2,1,0:T(8,128)(2,1)} %copy-done.9, bf16[2,128,256]{2,1,0:T(8,128)(2,1)} %copy-done.10, bf16[2,128,256]{2,1,0:T(8,128)(2,1)} %copy-done.11, ...), custom_call_target="tpu_custom_call" | custom-call | tf_op jit(solution)/shard_map/pallas_call | solution.py:239
  192.6 1.2 collective-permute-start.35
  193.8 7.0 %shard_map.58 = f32[128,3072]{1,0:T(8,128)} custom-call(s32[2]{0:T(128)} %pad_add_fusion.where_ref, bf16[2,128,256]{2,1,0:T(8,128)(2,1)} %get-tuple-element.37.refs_0_, bf16[2,128,256]{2,1,0:T(8,128)(2,1)} %copy-done.9, bf16[2,128,256]{2,1,0:T(8,128)(2,1)} %copy-done.10, bf16[2,128,256]{2,1,0:T(8,128)(2,1)} %copy-done.11, ...), custom_call_target="tpu_custom_call" | custom-call | tf_op jit(solution)/shard_map/pallas_call | solution.py:239
  200.8 11.6 %collective-permute-done.35 = bf16[128,3072]{1,0:T(8,128)(2,1)S(1)} collective-permute-done((bf16[128,3072]{1,0:T(8,128)(2,1)}, bf16[128,3072]{1,0:T(8,128)(2,1)S(1)}, u32[]{:S(2)}, u32[]{:S(2)}) %collective-permute-start.35) | collective-permute-done | bytes 786464 | tf_op jit(solution)/shard_map/ppermute | solution.py:196
  212.4 2.4 %fusion = bf16[1,128,3072]{2,1,0:T(8,128)(2,1)} fusion(f32[128,3072]{1,0:T(8,128)} %shard_map.58, bf16[128,3072]{1,0:T(8,128)(2,1)S(1)} %collective-permute-done.35), kind=kLoop, calls=%fused_computation.1 | loop fusion | flops 1179648 | bytes 3145728 | tf_op jit(solution)/shard_map/broadcast_in_dim | solution.py:252
  (89 shorter events, 1.4 us)
Async XLA Ops:
  4.0 9.7 %collective-permute-start.10 = (bf16[3,128,128]{2,1,0:T(8,128)(2,1)}, bf16[3,128,128]{2,1,0:T(8,128)(2,1)S(1)}, u32[]{:S(2)}, u32[]{:S(2)}) collective-permute-start(bf16[3,128,128]{2,1,0:T(8,128)(2,1)} %get-tuple-element.42), channel_id=1, source_target_pairs={{0,4},{4,8},{8,12},{12,0},{16,20},{20,24},{24,28},{28,16},{1,5},{5... | collective-permute-start | bytes 294920 | tf_op jit(solution)/shard_map/ppermute | solution.py:196
  7.1 90.3 %collective-permute-start.21 = (bf16[384,768]{1,0:T(8,128)(2,1)S(1)}, bf16[384,768]{1,0:T(8,128)(2,1)S(1)}, u32[]{:S(2)}, u32[]{:S(2)}) collective-permute-start(bf16[384,768]{1,0:T(8,128)(2,1)S(1)} %copy-done), channel_id=1, source_target_pairs={{0,8},{4,12},{8,0},{12,4},{1,9},{5,13},{9,1},{13,5},{2,10},{6,14},... | collective-permute-start | bytes 1769480 | tf_op jit(solution)/shard_map/ppermute | solution.py:209
  9.7 34.1 %collective-permute-start.11 = (bf16[3,128,128]{2,1,0:T(8,128)(2,1)}, bf16[3,128,128]{2,1,0:T(8,128)(2,1)S(1)}, u32[]{:S(2)}, u32[]{:S(2)}) collective-permute-start(bf16[3,128,128]{2,1,0:T(8,128)(2,1)} %get-tuple-element.43), channel_id=1, source_target_pairs={{0,8},{4,12},{8,0},{12,4},{16,24},{20,28},{24,16},{28,20},{1,9},{5... | collective-permute-start | bytes 294920 | tf_op jit(solution)/shard_map/ppermute | solution.py:196
  10.0 34.4 %collective-permute-start.12 = (bf16[3,128,128]{2,1,0:T(8,128)(2,1)}, bf16[3,128,128]{2,1,0:T(8,128)(2,1)S(1)}, u32[]{:S(2)}, u32[]{:S(2)}) collective-permute-start(bf16[3,128,128]{2,1,0:T(8,128)(2,1)} %get-tuple-element.44), channel_id=1, source_target_pairs={{0,12},{4,0},{8,4},{12,8},{16,28},{20,16},{24,20},{28,24},{1,13},{... | collective-permute-start | bytes 294920 | tf_op jit(solution)/shard_map/ppermute | solution.py:196
  12.1 35.3 %collective-permute-start.13 = (bf16[3,128,128]{2,1,0:T(8,128)(2,1)}, bf16[3,128,128]{2,1,0:T(8,128)(2,1)S(1)}, u32[]{:S(2)}, u32[]{:S(2)}) collective-permute-start(bf16[3,128,128]{2,1,0:T(8,128)(2,1)} %get-tuple-element.45), channel_id=1, source_target_pairs={{0,16},{4,20},{8,24},{12,28},{16,0},{20,4},{24,8},{28,12},{1,17},{... | collective-permute-start | bytes 294920 | tf_op jit(solution)/shard_map/ppermute | solution.py:196
  13.7 42.1 %copy-start.21 = (bf16[3,128,128]{2,1,0:T(8,128)(2,1)}, bf16[3,128,128]{2,1,0:T(8,128)(2,1)S(1)}, u32[]{:S(2)}) copy-start(bf16[3,128,128]{2,1,0:T(8,128)(2,1)S(1)} %collective-permute-done.10.refs_1_) | copy-start | bytes 294916
  13.7 34.3 %collective-permute-start.14 = (bf16[3,128,128]{2,1,0:T(8,128)(2,1)}, bf16[3,128,128]{2,1,0:T(8,128)(2,1)S(1)}, u32[]{:S(2)}, u32[]{:S(2)}) collective-permute-start(bf16[3,128,128]{2,1,0:T(8,128)(2,1)} %get-tuple-element.46), channel_id=1, source_target_pairs={{0,20},{4,24},{8,28},{12,16},{16,4},{20,8},{24,12},{28,0},{1,21},{... | collective-permute-start | bytes 294920 | tf_op jit(solution)/shard_map/ppermute | solution.py:196
  43.8 12.1 %copy-start.22 = (bf16[3,128,128]{2,1,0:T(8,128)(2,1)}, bf16[3,128,128]{2,1,0:T(8,128)(2,1)S(1)}, u32[]{:S(2)}) copy-start(bf16[3,128,128]{2,1,0:T(8,128)(2,1)S(1)} %collective-permute-done.11.refs_2_) | copy-start | bytes 294916
  43.8 9.7 %collective-permute-start.15 = (bf16[3,128,128]{2,1,0:T(8,128)(2,1)}, bf16[3,128,128]{2,1,0:T(8,128)(2,1)S(1)}, u32[]{:S(2)}, u32[]{:S(2)}) collective-permute-start(bf16[3,128,128]{2,1,0:T(8,128)(2,1)} %get-tuple-element.47), channel_id=1, source_target_pairs={{0,24},{4,28},{8,16},{12,20},{16,8},{20,12},{24,0},{28,4},{1,25},{... | collective-permute-start | bytes 294920 | tf_op jit(solution)/shard_map/ppermute | solution.py:196
  44.4 11.5 %collective-permute-start.16 = (bf16[3,128,128]{2,1,0:T(8,128)(2,1)}, bf16[3,128,128]{2,1,0:T(8,128)(2,1)S(1)}, u32[]{:S(2)}, u32[]{:S(2)}) collective-permute-start(bf16[3,128,128]{2,1,0:T(8,128)(2,1)} %get-tuple-element.48), channel_id=1, source_target_pairs={{0,28},{4,16},{8,20},{12,24},{16,12},{20,0},{24,4},{28,8},{1,29},{... | collective-permute-start | bytes 294920 | tf_op jit(solution)/shard_map/ppermute | solution.py:196
  47.4 31.7 %collective-permute-start = (bf16[3,128,256]{2,1,0:T(8,128)(2,1)}, bf16[3,128,256]{2,1,0:T(8,128)(2,1)S(1)}, u32[]{:S(2)}, u32[]{:S(2)}) collective-permute-start(bf16[3,128,256]{2,1,0:T(8,128)(2,1)} %get-tuple-element.30), channel_id=1, source_target_pairs={{0,4},{4,8},{8,12},{12,0},{16,20},{20,24},{24,28},{28,16},{1,5},{5... | collective-permute-start | bytes 589832 | tf_op jit(solution)/shard_map/ppermute | solution.py:196
  48.0 32.9 %collective-permute-start.1 = (bf16[3,128,256]{2,1,0:T(8,128)(2,1)}, bf16[3,128,256]{2,1,0:T(8,128)(2,1)S(1)}, u32[]{:S(2)}, u32[]{:S(2)}) collective-permute-start(bf16[3,128,256]{2,1,0:T(8,128)(2,1)} %get-tuple-element.31), channel_id=1, source_target_pairs={{0,8},{4,12},{8,0},{12,4},{16,24},{20,28},{24,16},{28,20},{1,9},{5... | collective-permute-start | bytes 589832 | tf_op jit(solution)/shard_map/ppermute | solution.py:196
  61.3 10.5 %collective-permute-start.17 = (bf16[2,128,128]{2,1,0:T(8,128)(2,1)}, bf16[2,128,128]{2,1,0:T(8,128)(2,1)S(1)}, u32[]{:S(2)}, u32[]{:S(2)}) collective-permute-start(bf16[2,128,128]{2,1,0:T(8,128)(2,1)} %get-tuple-element.50), channel_id=1, source_target_pairs={{0,12},{4,0},{8,4},{12,8},{16,28},{20,16},{24,20},{28,24},{1,13},{... | collective-permute-start | bytes 196616 | tf_op jit(solution)/shard_map/ppermute | solution.py:196
  61.5 20.8 %collective-permute-start.2 = (bf16[3,128,256]{2,1,0:T(8,128)(2,1)}, bf16[3,128,256]{2,1,0:T(8,128)(2,1)S(1)}, u32[]{:S(2)}, u32[]{:S(2)}) collective-permute-start(bf16[3,128,256]{2,1,0:T(8,128)(2,1)} %get-tuple-element.32), channel_id=1, source_target_pairs={{0,12},{4,0},{8,4},{12,8},{16,28},{20,16},{24,20},{28,24},{1,13},{... | collective-permute-start | bytes 589832 | tf_op jit(solution)/shard_map/ppermute | solution.py:196
  71.8 25.6 %copy-start.12 = (bf16[2,128,128]{2,1,0:T(8,128)(2,1)}, bf16[2,128,128]{2,1,0:T(8,128)(2,1)S(1)}, u32[]{:S(2)}) copy-start(bf16[2,128,128]{2,1,0:T(8,128)(2,1)S(1)} %collective-permute-done.17.refs_5_) | copy-start | bytes 196612
  71.8 5.4 %collective-permute-start.18 = (bf16[2,128,128]{2,1,0:T(8,128)(2,1)}, bf16[2,128,128]{2,1,0:T(8,128)(2,1)S(1)}, u32[]{:S(2)}, u32[]{:S(2)}) collective-permute-start(bf16[2,128,128]{2,1,0:T(8,128)(2,1)} %get-tuple-element.51), channel_id=1, source_target_pairs={{0,8},{4,12},{8,0},{12,4},{16,24},{20,28},{24,16},{28,20},{1,9},{5... | collective-permute-start | bytes 196616 | tf_op jit(solution)/shard_map/ppermute | solution.py:196
  77.2 22.2 %copy-start.13 = (bf16[2,128,128]{2,1,0:T(8,128)(2,1)}, bf16[2,128,128]{2,1,0:T(8,128)(2,1)S(1)}, u32[]{:S(2)}) copy-start(bf16[2,128,128]{2,1,0:T(8,128)(2,1)S(1)} %collective-permute-done.18.refs_6_) | copy-start | bytes 196612
  77.2 18.5 %collective-permute-start.3 = (bf16[3,128,256]{2,1,0:T(8,128)(2,1)}, bf16[3,128,256]{2,1,0:T(8,128)(2,1)S(1)}, u32[]{:S(2)}, u32[]{:S(2)}) collective-permute-start(bf16[3,128,256]{2,1,0:T(8,128)(2,1)} %get-tuple-element.33), channel_id=1, source_target_pairs={{0,16},{4,20},{8,24},{12,28},{16,0},{20,4},{24,8},{28,12},{1,17},{... | collective-permute-start | bytes 589832 | tf_op jit(solution)/shard_map/ppermute | solution.py:196
  79.1 18.1 %collective-permute-start.4 = (bf16[3,128,256]{2,1,0:T(8,128)(2,1)}, bf16[3,128,256]{2,1,0:T(8,128)(2,1)S(1)}, u32[]{:S(2)}, u32[]{:S(2)}) collective-permute-start(bf16[3,128,256]{2,1,0:T(8,128)(2,1)} %get-tuple-element.34), channel_id=1, source_target_pairs={{0,20},{4,24},{8,28},{12,16},{16,4},{20,8},{24,12},{28,0},{1,21},{... | collective-permute-start | bytes 589832 | tf_op jit(solution)/shard_map/ppermute | solution.py:196
  80.9 16.4 %collective-permute-start.5 = (bf16[3,128,256]{2,1,0:T(8,128)(2,1)}, bf16[3,128,256]{2,1,0:T(8,128)(2,1)S(1)}, u32[]{:S(2)}, u32[]{:S(2)}) collective-permute-start(bf16[3,128,256]{2,1,0:T(8,128)(2,1)} %get-tuple-element.35), channel_id=1, source_target_pairs={{0,24},{4,28},{8,16},{12,20},{16,8},{20,12},{24,0},{28,4},{1,25},{... | collective-permute-start | bytes 589832 | tf_op jit(solution)/shard_map/ppermute | solution.py:196
  82.2 17.2 %copy-start.16 = (bf16[3,128,256]{2,1,0:T(8,128)(2,1)}, bf16[3,128,256]{2,1,0:T(8,128)(2,1)S(1)}, u32[]{:S(2)}) copy-start(bf16[3,128,256]{2,1,0:T(8,128)(2,1)S(1)} %collective-permute-done.2.refs_3_) | copy-start | bytes 589828
  82.2 17.2 %collective-permute-start.6 = (bf16[3,128,256]{2,1,0:T(8,128)(2,1)}, bf16[3,128,256]{2,1,0:T(8,128)(2,1)S(1)}, u32[]{:S(2)}, u32[]{:S(2)}) collective-permute-start(bf16[3,128,256]{2,1,0:T(8,128)(2,1)} %get-tuple-element.36), channel_id=1, source_target_pairs={{0,28},{4,16},{8,20},{12,24},{16,12},{20,0},{24,4},{28,8},{1,29},{... | collective-permute-start | bytes 589832 | tf_op jit(solution)/shard_map/ppermute | solution.py:196
  95.7 46.1 %collective-permute-start.27 = (bf16[384,768]{1,0:T(8,128)(2,1)S(1)}, bf16[384,768]{1,0:T(8,128)(2,1)S(1)}, u32[]{:S(2)}, u32[]{:S(2)}) collective-permute-start(bf16[384,768]{1,0:T(8,128)(2,1)S(1)} %copy-done), channel_id=1, source_target_pairs={{0,2},{1,3},{2,0},{3,1},{4,6},{5,7},{6,4},{7,5},{8,10},{9,11},{10,... | collective-permute-start | bytes 1769480 | tf_op jit(solution)/shard_map/ppermute | solution.py:219
  97.2 52.7 %collective-permute-start.23 = (bf16[384,768]{1,0:T(8,128)(2,1)S(1)}, bf16[384,768]{1,0:T(8,128)(2,1)S(1)}, u32[]{:S(2)}, u32[]{:S(2)}) collective-permute-start(bf16[384,768]{1,0:T(8,128)(2,1)S(1)} %copy-done), channel_id=1, source_target_pairs={{0,1},{1,0},{2,3},{3,2},{4,5},{5,4},{6,7},{7,6},{8,9},{9,8},{10,11... | collective-permute-start | bytes 1769480 | tf_op jit(solution)/shard_map/ppermute | solution.py:219
  97.3 52.7 %collective-permute-start.20 = (bf16[384,768]{1,0:T(8,128)(2,1)S(1)}, bf16[384,768]{1,0:T(8,128)(2,1)S(1)}, u32[]{:S(2)}, u32[]{:S(2)}) collective-permute-start(bf16[384,768]{1,0:T(8,128)(2,1)S(1)} %copy-done), channel_id=1, source_target_pairs={{0,4},{4,0},{8,12},{12,8},{1,5},{5,1},{9,13},{13,9},{2,6},{6,2},{1... | collective-permute-start | bytes 1769480 | tf_op jit(solution)/shard_map/ppermute | solution.py:209
  97.4 88.4 %copy-start.1 = (bf16[384,768]{1,0:T(8,128)(2,1)}, bf16[384,768]{1,0:T(8,128)(2,1)S(1)}, u32[]{:S(2)}) copy-start(bf16[384,768]{1,0:T(8,128)(2,1)S(1)} %collective-permute-done.21.refs_10_) | copy-start | bytes 1769476
  97.4 53.3 %collective-permute-start.22 = (bf16[384,768]{1,0:T(8,128)(2,1)S(1)}, bf16[384,768]{1,0:T(8,128)(2,1)S(1)}, u32[]{:S(2)}, u32[]{:S(2)}) collective-permute-start(bf16[384,768]{1,0:T(8,128)(2,1)S(1)} %collective-permute-done.21.refs_10_), channel_id=1, source_target_pairs={{0,4},{4,0},{8,12},{12,8},{1,5},{5,1},{9,13},{13,9},{2,6},{6,2},{1... | collective-permute-start | bytes 1769480 | tf_op jit(solution)/shard_map/ppermute | solution.py:209
  99.5 27.8 %collective-permute-start.19 = (bf16[2,128,128]{2,1,0:T(8,128)(2,1)}, bf16[2,128,128]{2,1,0:T(8,128)(2,1)}, u32[]{:S(2)}, u32[]{:S(2)}) collective-permute-start(bf16[2,128,128]{2,1,0:T(8,128)(2,1)} %get-tuple-element.52), channel_id=1, source_target_pairs={{0,4},{4,8},{8,12},{12,0},{16,20},{20,24},{24,28},{28,16},{1,5},{5... | collective-permute-start | bytes 196616 | tf_op jit(solution)/shard_map/ppermute | solution.py:196
  127.3 5.2 %collective-permute-start.7 = (bf16[2,128,256]{2,1,0:T(8,128)(2,1)}, bf16[2,128,256]{2,1,0:T(8,128)(2,1)S(1)}, u32[]{:S(2)}, u32[]{:S(2)}) collective-permute-start(bf16[2,128,256]{2,1,0:T(8,128)(2,1)} %get-tuple-element.38), channel_id=1, source_target_pairs={{0,12},{4,0},{8,4},{12,8},{16,28},{20,16},{24,20},{28,24},{1,13},{... | collective-permute-start | bytes 393224 | tf_op jit(solution)/shard_map/ppermute | solution.py:196
  132.5 8.7 %collective-permute-start.8 = (bf16[2,128,256]{2,1,0:T(8,128)(2,1)}, bf16[2,128,256]{2,1,0:T(8,128)(2,1)S(1)}, u32[]{:S(2)}, u32[]{:S(2)}) collective-permute-start(bf16[2,128,256]{2,1,0:T(8,128)(2,1)} %get-tuple-element.39), channel_id=1, source_target_pairs={{0,8},{4,12},{8,0},{12,4},{16,24},{20,28},{24,16},{28,20},{1,9},{5... | collective-permute-start | bytes 393224 | tf_op jit(solution)/shard_map/ppermute | solution.py:196
  141.2 7.0 %collective-permute-start.9 = (bf16[2,128,256]{2,1,0:T(8,128)(2,1)}, bf16[2,128,256]{2,1,0:T(8,128)(2,1)S(1)}, u32[]{:S(2)}, u32[]{:S(2)}) collective-permute-start(bf16[2,128,256]{2,1,0:T(8,128)(2,1)} %get-tuple-element.40), channel_id=1, source_target_pairs={{0,4},{4,8},{8,12},{12,0},{16,20},{20,24},{24,28},{28,16},{1,5},{5... | collective-permute-start | bytes 393224 | tf_op jit(solution)/shard_map/ppermute | solution.py:196
  141.9 44.0 %copy-start.2 = (bf16[384,768]{1,0:T(8,128)(2,1)}, bf16[384,768]{1,0:T(8,128)(2,1)S(1)}, u32[]{:S(2)}) copy-start(bf16[384,768]{1,0:T(8,128)(2,1)S(1)} %collective-permute-done.27.refs_16_) | copy-start | bytes 1769476
  141.9 10.3 %collective-permute-start.31 = (bf16[384,768]{1,0:T(8,128)(2,1)S(1)}, bf16[384,768]{1,0:T(8,128)(2,1)S(1)}, u32[]{:S(2)}, u32[]{:S(2)}) collective-permute-start(bf16[384,768]{1,0:T(8,128)(2,1)S(1)} %collective-permute-done.27.refs_16_), channel_id=1, source_target_pairs={{0,1},{1,0},{2,3},{3,2},{4,5},{5,4},{6,7},{7,6},{8,9},{9,8},{10,11... | collective-permute-start | bytes 1769480 | tf_op jit(solution)/shard_map/ppermute | solution.py:219
  148.2 15.2 %collective-permute-start.29 = (bf16[384,768]{1,0:T(8,128)(2,1)S(1)}, bf16[384,768]{1,0:T(8,128)(2,1)}, u32[]{:S(2)}, u32[]{:S(2)}) collective-permute-start(bf16[384,768]{1,0:T(8,128)(2,1)S(1)} %collective-permute-done.21.refs_10_), channel_id=1, source_target_pairs={{0,2},{1,3},{2,0},{3,1},{4,6},{5,7},{6,4},{7,5},{8,10},{9,11},{10,... | collective-permute-start | bytes 1769480 | tf_op jit(solution)/shard_map/ppermute | solution.py:219
  149.9 35.9 %copy-start.3 = (bf16[384,768]{1,0:T(8,128)(2,1)}, bf16[384,768]{1,0:T(8,128)(2,1)S(1)}, u32[]{:S(2)}) copy-start(bf16[384,768]{1,0:T(8,128)(2,1)S(1)} %collective-permute-done.23.refs_12_) | copy-start | bytes 1769476
  149.9 13.5 %collective-permute-start.25 = (bf16[384,768]{1,0:T(8,128)(2,1)S(1)}, bf16[384,768]{1,0:T(8,128)(2,1)S(1)}, u32[]{:S(2)}, u32[]{:S(2)}) collective-permute-start(bf16[384,768]{1,0:T(8,128)(2,1)S(1)} %collective-permute-done.21.refs_10_), channel_id=1, source_target_pairs={{0,1},{1,0},{2,3},{3,2},{4,5},{5,4},{6,7},{7,6},{8,9},{9,8},{10,11... | collective-permute-start | bytes 1769480 | tf_op jit(solution)/shard_map/ppermute | solution.py:219
  150.0 35.8 %copy-start.4 = (bf16[384,768]{1,0:T(8,128)(2,1)}, bf16[384,768]{1,0:T(8,128)(2,1)S(1)}, u32[]{:S(2)}) copy-start(bf16[384,768]{1,0:T(8,128)(2,1)S(1)} %collective-permute-done.20.refs_9_) | copy-start | bytes 1769476
  150.0 26.1 %collective-permute-start.28 = (bf16[384,768]{1,0:T(8,128)(2,1)S(1)}, bf16[384,768]{1,0:T(8,128)(2,1)S(1)}, u32[]{:S(2)}, u32[]{:S(2)}) collective-permute-start(bf16[384,768]{1,0:T(8,128)(2,1)S(1)} %collective-permute-done.20.refs_9_), channel_id=1, source_target_pairs={{0,2},{1,3},{2,0},{3,1},{4,6},{5,7},{6,4},{7,5},{8,10},{9,11},{10,... | collective-permute-start | bytes 1769480 | tf_op jit(solution)/shard_map/ppermute | solution.py:219
  150.7 35.2 %copy-start.5 = (bf16[384,768]{1,0:T(8,128)(2,1)}, bf16[384,768]{1,0:T(8,128)(2,1)S(1)}, u32[]{:S(2)}) copy-start(bf16[384,768]{1,0:T(8,128)(2,1)S(1)} %collective-permute-done.22.refs_11_) | copy-start | bytes 1769476
  150.7 32.8 %collective-permute-start.30 = (bf16[384,768]{1,0:T(8,128)(2,1)S(1)}, bf16[384,768]{1,0:T(8,128)(2,1)}, u32[]{:S(2)}, u32[]{:S(2)}) collective-permute-start(bf16[384,768]{1,0:T(8,128)(2,1)S(1)} %collective-permute-done.22.refs_11_), channel_id=1, source_target_pairs={{0,2},{1,3},{2,0},{3,1},{4,6},{5,7},{6,4},{7,5},{8,10},{9,11},{10,... | collective-permute-start | bytes 1769480 | tf_op jit(solution)/shard_map/ppermute | solution.py:219
  152.1 31.3 %copy-start.6 = (bf16[384,768]{1,0:T(8,128)(2,1)}, bf16[384,768]{1,0:T(8,128)(2,1)S(1)}, u32[]{:S(2)}) copy-start(bf16[384,768]{1,0:T(8,128)(2,1)S(1)} %collective-permute-done.31.refs_20_) | copy-start | bytes 1769476
  152.1 32.0 %collective-permute-start.24 = (bf16[384,768]{1,0:T(8,128)(2,1)S(1)}, bf16[384,768]{1,0:T(8,128)(2,1)}, u32[]{:S(2)}, u32[]{:S(2)}) collective-permute-start(bf16[384,768]{1,0:T(8,128)(2,1)S(1)} %collective-permute-done.20.refs_9_), channel_id=1, source_target_pairs={{0,1},{1,0},{2,3},{3,2},{4,5},{5,4},{6,7},{7,6},{8,9},{9,8},{10,11... | collective-permute-start | bytes 1769480 | tf_op jit(solution)/shard_map/ppermute | solution.py:219
  163.4 20.7 %collective-permute-start.26 = (bf16[384,768]{1,0:T(8,128)(2,1)S(1)}, bf16[384,768]{1,0:T(8,128)(2,1)}, u32[]{:S(2)}, u32[]{:S(2)}) collective-permute-start(bf16[384,768]{1,0:T(8,128)(2,1)S(1)} %collective-permute-done.22.refs_11_), channel_id=1, source_target_pairs={{0,1},{1,0},{2,3},{3,2},{4,5},{5,4},{6,7},{7,6},{8,9},{9,8},{10,11... | collective-permute-start | bytes 1769480 | tf_op jit(solution)/shard_map/ppermute | solution.py:219
  163.4 20.0 %copy-start.7 = (bf16[384,768]{1,0:T(8,128)(2,1)}, bf16[384,768]{1,0:T(8,128)(2,1)S(1)}, u32[]{:S(2)}) copy-start(bf16[384,768]{1,0:T(8,128)(2,1)S(1)} %collective-permute-done.25.refs_14_) | copy-start | bytes 1769476
  163.4 20.7 %collective-permute-start.33 = (bf16[384,768]{1,0:T(8,128)(2,1)}, bf16[384,768]{1,0:T(8,128)(2,1)}, u32[]{:S(2)}, u32[]{:S(2)}) collective-permute-start(bf16[384,768]{1,0:T(8,128)(2,1)} %collective-permute-done.29.refs_18_), channel_id=1, source_target_pairs={{0,1},{1,0},{2,3},{3,2},{4,5},{5,4},{6,7},{7,6},{8,9},{9,8},{10,11... | collective-permute-start | bytes 1769480 | tf_op jit(solution)/shard_map/ppermute | solution.py:219
  176.1 8.1 %collective-permute-start.32 = (bf16[384,768]{1,0:T(8,128)(2,1)S(1)}, bf16[384,768]{1,0:T(8,128)(2,1)}, u32[]{:S(2)}, u32[]{:S(2)}) collective-permute-start(bf16[384,768]{1,0:T(8,128)(2,1)S(1)} %collective-permute-done.28.refs_17_), channel_id=1, source_target_pairs={{0,1},{1,0},{2,3},{3,2},{4,5},{5,4},{6,7},{7,6},{8,9},{9,8},{10,11... | collective-permute-start | bytes 1769480 | tf_op jit(solution)/shard_map/ppermute | solution.py:219
  183.5 2.3 %collective-permute-start.34 = (bf16[384,768]{1,0:T(8,128)(2,1)}, bf16[384,768]{1,0:T(8,128)(2,1)}, u32[]{:S(2)}, u32[]{:S(2)}) collective-permute-start(bf16[384,768]{1,0:T(8,128)(2,1)} %collective-permute-done.30.refs_19_), channel_id=1, source_target_pairs={{0,1},{1,0},{2,3},{3,2},{4,5},{5,4},{6,7},{7,6},{8,9},{9,8},{10,11... | collective-permute-start | bytes 1769480 | tf_op jit(solution)/shard_map/ppermute | solution.py:219
  192.6 19.8 %collective-permute-start.35 = (bf16[128,3072]{1,0:T(8,128)(2,1)}, bf16[128,3072]{1,0:T(8,128)(2,1)S(1)}, u32[]{:S(2)}, u32[]{:S(2)}) collective-permute-start(bf16[128,3072]{1,0:T(8,128)(2,1)} %shard_map.59), channel_id=1, source_target_pairs={{0,16},{4,20},{8,24},{12,28},{16,0},{20,4},{24,8},{28,12},{1,17},{... | collective-permute-start | bytes 2359304 | tf_op jit(solution)/shard_map/ppermute | solution.py:196
  (16 other events, 75.8 us)

commit v3 on v2

--- a/solution.py
+++ b/solution.py
@@ -135,24 +135,40 @@
             outs[j % n_tensor][j // n_tensor, :, cols] = mixed.astype(jnp.bfloat16)
 
 
-def project_kernel(where_ref, *refs, row_set, n_tensor, n_bucket):
+def project_kernel(where_ref, *refs, row_set, n_tensor, n_bucket, parts):
     *ins, out_ref, o_scr = refs
-    pieces, weights = ins[: -n_bucket * n_tensor], ins[-n_bucket * n_tensor :]
+    n_weights = n_bucket * len(parts)
+    pieces, weights = ins[:-n_weights], ins[-n_weights:]
     width = weights[0].shape[1]
     z, b = where_ref[0], where_ref[1]
     for c, (lo, hi) in enumerate(head_chunks(o_scr.shape[-1])):
         for dz in range(n_tensor):
             o_scr[lax.rem(z + dz, n_tensor), :, lo:hi] = pieces[c * n_tensor + dz][row_set]
-    for dz in range(n_tensor):
+    for i, e in enumerate(parts):
         acc = None
         for m in range(n_bucket):
             part = jnp.dot(
-                o_scr[jnp.bitwise_xor(b, m)], weights[m * n_tensor + dz][...],
+                o_scr[jnp.bitwise_xor(b, m)], weights[i * n_bucket + m][...],
                 preferred_element_type=jnp.float32,
             )
             acc = part if acc is None else acc + part
-        place = pl.multiple_of(jnp.bitwise_xor(z, dz) * width, HS)
-        out_ref[:, pl.ds(place, width)] = acc.astype(out_ref.dtype)
+        slot = jnp.bitwise_and(jnp.bitwise_xor(z, e), len(parts) - 1)
+        out_ref[:, pl.ds(pl.multiple_of(slot * width, HS), width)] = acc.astype(out_ref.dtype)
+
+
+def finish_kernel(where_ref, own_ref, *refs, n_tensor):
+    *others, out_ref = refs
+    width = others[0].shape[1]
+    n_groups = own_ref.shape[1] // width
+    per = n_tensor // n_groups
+    for g in range(n_groups):
+        first = jnp.bitwise_xor(where_ref[0], g * per)
+        first = first - jnp.bitwise_and(first, per - 1)
+        cols = pl.ds(pl.multiple_of(first * (width // per), HS), width)
+        acc = own_ref[:, cols]
+        for other in others[g::n_groups]:
+            acc = acc + other[...].astype(jnp.float32)
+        out_ref[:, cols] = acc.astype(out_ref.dtype)
 
 
 def vmem_call(kernel, n_in, out_shape, scratch=()):
@@ -218,7 +234,6 @@
             for w in held[m]:
                 held[m ^ bit].append(lax.ppermute(w, "bucket", swap))
         bit //= 2
-    flat_weights = [w for m in range(n_bucket) for w in held[m]]
 
     pos = jnp.stack(
         [((s - ds) % n_seq * n_tensor + (z - dz) % n_tensor) * rows for ds, dz in shifts]
@@ -235,21 +250,34 @@
         pieces.append(mixed[0])
         pieces += [shifted(mixed[dz], 0, -dz) for dz in range(1, n_tensor)]
 
-    def project(row_set, dtype):
+    where = jnp.stack([z, b])
+
+    def project(row_set, dtype, parts):
+        weights = [held[m][e] for e in parts for m in range(n_bucket)]
         return vmem_call(
             functools.partial(
-                project_kernel, row_set=row_set, n_tensor=n_tensor, n_bucket=n_bucket
+                project_kernel, row_set=row_set, n_tensor=n_tensor, n_bucket=n_bucket, parts=parts
             ),
-            len(pieces) + n_tensor * n_bucket,
-            [jax.ShapeDtypeStruct((rows, model), dtype)],
+            len(pieces) + len(weights),
+            [jax.ShapeDtypeStruct((rows, len(parts) * out_weight.shape[1]), dtype)],
             [pltpu.VMEM((n_tensor, rows, width), bf16)],
-        )(jnp.stack([z, b]), *pieces, *flat_weights)[0]
-
-    received = [shifted(project(ds, bf16), -ds, 0) for ds in range(1, n_seq)]
-    summed = project(0, f32)
-    for other in received:
-        summed = summed + other.astype(f32)
-    return summed.astype(bf16)[None]
+        )(where, *pieces, *weights)[0]
+
+    per = n_tensor // 2
+    received = [
+        shifted(
+            project(ds, bf16, tuple(range(g * per, (g + 1) * per))),
+            -ds, 0,
+        )
+        for ds in range(1, n_seq)
+        for g in range(2)
+    ]
+    own = project(0, f32, tuple(range(n_tensor)))
+    return vmem_call(
+        functools.partial(finish_kernel, n_tensor=n_tensor),
+        1 + len(received),
+        [jax.ShapeDtypeStruct((rows, own.shape[1]), bf16)],
+    )(where, own, *received)[0][None]
 
 
 def solution(mesh):
@@ -261,6 +289,7 @@
             heads % (n_seq * n_tensor) == 0
             and n_tensor == n_bucket
             and 1 < n_bucket
+            and 1 < n_seq
             and n_bucket & (n_bucket - 1) == 0
         )
         step = jax.shard_map(

time: 215 us -> 206 us (0.958)
  waiting for transfers between devices: 121 us -> 103 us
  starting transfers between devices: 56.6 us -> 63.9 us
  Pallas kernels: 30 us -> 34.7 us
  other arithmetic: 3.09 us -> 0.58 us
    ppermute x21 -> x22, waiting for transfers between devices: 88.7 us -> 73.4 us  [shifted(): return lax.ppermute(x, ('seq', 'tensor'), perm)]
    ppermute x21 -> x22, starting transfers between devices: 46 us -> 53.1 us  [shifted(): return lax.ppermute(x, ('seq', 'tensor'), perm)]
    ppermute x12, waiting for transfers between devices: 32.5 us -> 29.2 us  [head_step(): held[m ^ bit].append(lax.ppermute(w, 'bucket', swap))]
    pallas_call x0 -> x1, Pallas kernels: none -> 2.61 us  [head_step(): vmem_call(functools.partial(finish_kernel, n_tensor=n_tensor), 1 + len(re...]
    broadcast_in_dim x1 -> x0, other arithmetic: 2.44 us -> none  [head_step(): return summed.astype(bf16)[None]]
    pallas_call x2 -> x3, Pallas kernels: 13.7 us -> 15.8 us  [project(): vmem_call(functools.partial(project_kernel, row_set=row_set, n_tensor=n_t...]
  transfers between devices with their start and end apart: 36 -> 37, of which waited for: 15 -> 14; matrix products, arithmetic and copies ran while one was open for 1% -> 1% of each run, Pallas kernels for 9% -> 14%
where the time goes in v3:
time: 206 us
  waiting for transfers between devices  103 us (50%)
  starting transfers between devices  63.9 us (31%)
  Pallas kernels  34.7 us (17%)
  local copies, waits for them, and re-layouts  3.27 us (2%)
    ppermute x22, waiting for transfers between devices, shifted(): return lax.ppermute(x, ('seq', 'tensor'), perm)  73.4 us
    ppermute x22, starting transfers between devices, shifted(): return lax.ppermute(x, ('seq', 'tensor'), perm)  53.1 us
    ppermute x12, waiting for transfers between devices, head_step(): held[m ^ bit].append(lax.ppermute(w, 'bucket', swap))  29.2 us
    pallas_call x3, Pallas kernels, project(): vmem_call(functools.partial(project_kernel, row_set=row_set, n_tensor=n_t...  15.8 us
    pallas_call x2, Pallas kernels, head_step(): vmem_call(functools.partial(attend_kernel, n_seq=n_seq, n_tensor=n_tensor...  12.9 us
    ppermute x12, starting transfers between devices, head_step(): held[m ^ bit].append(lax.ppermute(w, 'bucket', swap))  6.16 us
    ppermute x3, starting transfers between devices, head_step(): weights[e ^ bit] = lax.ppermute(weights[e], 'tensor', swap)  4.6 us
  transfers between devices with their start and end apart: 37, of which 14 were waited for; matrix products, arithmetic and copies ran while one was open for 1% of the time, Pallas kernels for 14%

profile of v3, /device:TPU:0, one launch (start us, length us, event | category | flops | bytes accessed | tf_op | source)
XLA Modules:
  0.0 205.9 jit_solution(8574694634397395056)
XLA Ops:
  0.0 0.6 stack.83.dest_ref
  0.6 3.4 %shard_map.55 = (bf16[3,128,256]{2,1,0:T(8,128)(2,1)}, bf16[3,128,256]{2,1,0:T(8,128)(2,1)}, bf16[3,128,256]{2,1,0:T(8,128)(2,1)}, bf16[3,128,256]{2,1,0:T(8,128...) custom-call(s32[8]{0:T(128)} %stack.83.dest_ref, ...), custom_call_target="tpu_custom_call" | custom-call | tf_op jit(solution)/shard_map/pallas_call | solution.py:200
  4.0 3.1 %collective-permute-start.10 = (bf16[3,128,128]{2,1,0:T(8,128)(2,1)}, bf16[3,128,128]{2,1,0:T(8,128)(2,1)S(1)}, u32[]{:S(2)}, u32[]{:S(2)}) collective-permute-start(bf16[3,128,128]{2,1,0:T(8,128)(2,1)} %get-tuple-element.42), channel_id=1, source_target_pairs={{0,4},{4,8},{8,12},{12,0},{16,20},{20,24},{24,28},{28,16},{1,5},{5... | collective-permute-start | bytes 294920 | tf_op jit(solution)/shard_map/ppermute | solution.py:212
  7.1 2.6 %collective-permute-start.27 = (bf16[384,768]{1,0:T(8,128)(2,1)S(1)}, bf16[384,768]{1,0:T(8,128)(2,1)S(1)}, u32[]{:S(2)}, u32[]{:S(2)}) collective-permute-start(bf16[384,768]{1,0:T(8,128)(2,1)S(1)} %copy-done), channel_id=1, source_target_pairs={{0,8},{4,12},{8,0},{12,4},{1,9},{5,13},{9,1},{13,5},{2,10},{6,14},... | collective-permute-start | bytes 1769480 | tf_op jit(solution)/shard_map/ppermute | solution.py:225
  10.0 2.1 %collective-permute-start.12 = (bf16[3,128,128]{2,1,0:T(8,128)(2,1)}, bf16[3,128,128]{2,1,0:T(8,128)(2,1)S(1)}, u32[]{:S(2)}, u32[]{:S(2)}) collective-permute-start(bf16[3,128,128]{2,1,0:T(8,128)(2,1)} %get-tuple-element.44), channel_id=1, source_target_pairs={{0,12},{4,0},{8,4},{12,8},{16,28},{20,16},{24,20},{28,24},{1,13},{... | collective-permute-start | bytes 294920 | tf_op jit(solution)/shard_map/ppermute | solution.py:212
  12.1 1.6 collective-permute-start.13
  13.8 15.5 %collective-permute-start.14 = (bf16[3,128,128]{2,1,0:T(8,128)(2,1)}, bf16[3,128,128]{2,1,0:T(8,128)(2,1)S(1)}, u32[]{:S(2)}, u32[]{:S(2)}) collective-permute-start(bf16[3,128,128]{2,1,0:T(8,128)(2,1)} %get-tuple-element.46), channel_id=1, source_target_pairs={{0,20},{4,24},{8,28},{12,16},{16,4},{20,8},{24,12},{28,0},{1,21},{... | collective-permute-start | bytes 294920 | tf_op jit(solution)/shard_map/ppermute | solution.py:212
  29.3 14.5 %collective-permute-done.11.refs_2_ = bf16[3,128,128]{2,1,0:T(8,128)(2,1)S(1)} collective-permute-done((bf16[3,128,128]{2,1,0:T(8,128)(2,1)}, bf16[3,128,128]{2,1,0:T(8,128)(2,1)S(1)}, u32[]{:S(2)}, u32[]{:S(2)}) %collective-permute-start.11) | collective-permute-done | bytes 98336 | tf_op jit(solution)/shard_map/ppermute | solution.py:212
  43.8 0.6 collective-permute-start.15
  44.4 3.0 %collective-permute-start.16 = (bf16[3,128,128]{2,1,0:T(8,128)(2,1)}, bf16[3,128,128]{2,1,0:T(8,128)(2,1)S(1)}, u32[]{:S(2)}, u32[]{:S(2)}) collective-permute-start(bf16[3,128,128]{2,1,0:T(8,128)(2,1)} %get-tuple-element.48), channel_id=1, source_target_pairs={{0,28},{4,16},{8,20},{12,24},{16,12},{20,0},{24,4},{28,8},{1,29},{... | collective-permute-start | bytes 294920 | tf_op jit(solution)/shard_map/ppermute | solution.py:212
  48.0 1.9 collective-permute-start.1
  50.6 0.7 stack.74.pos_ref
  51.3 2.3 %collective-permute-done.15.refs_6_ = bf16[3,128,128]{2,1,0:T(8,128)(2,1)S(1)} collective-permute-done((bf16[3,128,128]{2,1,0:T(8,128)(2,1)}, bf16[3,128,128]{2,1,0:T(8,128)(2,1)S(1)}, u32[]{:S(2)}, u32[]{:S(2)}) %collective-permute-start.15) | collective-permute-done | bytes 98336 | tf_op jit(solution)/shard_map/ppermute | solution.py:212
  53.5 2.4 %collective-permute-done.16.refs_7_ = bf16[3,128,128]{2,1,0:T(8,128)(2,1)S(1)} collective-permute-done((bf16[3,128,128]{2,1,0:T(8,128)(2,1)}, bf16[3,128,128]{2,1,0:T(8,128)(2,1)S(1)}, u32[]{:S(2)}, u32[]{:S(2)}) %collective-permute-start.16) | collective-permute-done | bytes 98336 | tf_op jit(solution)/shard_map/ppermute | solution.py:212
  55.9 0.6 copy-done.28
  56.5 4.8 %shard_map.57 = (bf16[2,128,128]{2,1,0:T(8,128)(2,1)}, bf16[2,128,128]{2,1,0:T(8,128)(2,1)}, bf16[2,128,128]{2,1,0:T(8,128)(2,1)}, bf16[2,128,128]{2,1,0:T(8,128)(2,1)}) custom-call(s32[9]{0:T(128)} %stack.74.pos_ref, bf16[3,128,128]{2,1,0:T(8,128)(2,1)} %get-tuple-element.41.refs_0_, bf16[3,128,128]{2,1,0:T(8,128)(2,1)} %copy-done.22, ...), custom_call_target="tpu_custom_call" | custom-call | tf_op jit(solution)/shard_map/pallas_call | solution.py:244
  61.5 7.7 %collective-permute-start.2 = (bf16[3,128,256]{2,1,0:T(8,128)(2,1)}, bf16[3,128,256]{2,1,0:T(8,128)(2,1)S(1)}, u32[]{:S(2)}, u32[]{:S(2)}) collective-permute-start(bf16[3,128,256]{2,1,0:T(8,128)(2,1)} %get-tuple-element.32), channel_id=1, source_target_pairs={{0,12},{4,0},{8,4},{12,8},{16,28},{20,16},{24,20},{28,24},{1,13},{... | collective-permute-start | bytes 589832 | tf_op jit(solution)/shard_map/ppermute | solution.py:212
  69.2 2.7 %collective-permute-done.17.refs_5_ = bf16[2,128,128]{2,1,0:T(8,128)(2,1)S(1)} collective-permute-done((bf16[2,128,128]{2,1,0:T(8,128)(2,1)}, bf16[2,128,128]{2,1,0:T(8,128)(2,1)S(1)}, u32[]{:S(2)}, u32[]{:S(2)}) %collective-permute-start.17) | collective-permute-done | bytes 65568 | tf_op jit(solution)/shard_map/ppermute | solution.py:212
  71.9 1.3 collective-permute-start.18
  73.1 4.1 %collective-permute-done.18.refs_6_ = bf16[2,128,128]{2,1,0:T(8,128)(2,1)S(1)} collective-permute-done((bf16[2,128,128]{2,1,0:T(8,128)(2,1)}, bf16[2,128,128]{2,1,0:T(8,128)(2,1)S(1)}, u32[]{:S(2)}, u32[]{:S(2)}) %collective-permute-start.18) | collective-permute-done | bytes 65568 | tf_op jit(solution)/shard_map/ppermute | solution.py:212
  77.2 1.9 collective-permute-start.3
  79.2 1.7 collective-permute-start.4
  80.9 1.4 collective-permute-start.5
  82.3 1.7 collective-permute-start.6
  84.0 11.6 %collective-permute-done.3.refs_4_ = bf16[3,128,256]{2,1,0:T(8,128)(2,1)S(1)} collective-permute-done((bf16[3,128,256]{2,1,0:T(8,128)(2,1)}, bf16[3,128,256]{2,1,0:T(8,128)(2,1)S(1)}, u32[]{:S(2)}, u32[]{:S(2)}) %collective-permute-start.3) | collective-permute-done | bytes 196640 | tf_op jit(solution)/shard_map/ppermute | solution.py:212
  95.6 1.6 collective-permute-start.21
  97.3 2.0 collective-permute-start.31
  100.0 8.1 %shard_map.56 = (bf16[2,128,256]{2,1,0:T(8,128)(2,1)}, bf16[2,128,256]{2,1,0:T(8,128)(2,1)}, bf16[2,128,256]{2,1,0:T(8,128)(2,1)}, bf16[2,128,256]{2,1,0:T(8,128)(2,1)}) custom-call(s32[9]{0:T(128)} %stack.74.pos_ref, bf16[3,128,256]{2,1,0:T(8,128)(2,1)} %get-tuple-element.29.refs_0_, bf16[3,128,256]{2,1,0:T(8,128)(2,1)} %copy-done.15, ...), custom_call_target="tpu_custom_call" | custom-call | tf_op jit(solution)/shard_map/pallas_call | solution.py:244
  108.1 12.8 %collective-permute-done.19.refs_7_ = bf16[2,128,128]{2,1,0:T(8,128)(2,1)} collective-permute-done((bf16[2,128,128]{2,1,0:T(8,128)(2,1)}, bf16[2,128,128]{2,1,0:T(8,128)(2,1)}, u32[]{:S(2)}, u32[]{:S(2)}) %collective-permute-start.19) | collective-permute-done | bytes 65568 | tf_op jit(solution)/shard_map/ppermute | solution.py:212
  120.9 5.1 %collective-permute-start.7 = (bf16[2,128,256]{2,1,0:T(8,128)(2,1)}, bf16[2,128,256]{2,1,0:T(8,128)(2,1)S(1)}, u32[]{:S(2)}, u32[]{:S(2)}) collective-permute-start(bf16[2,128,256]{2,1,0:T(8,128)(2,1)} %get-tuple-element.38), channel_id=1, source_target_pairs={{0,12},{4,0},{8,4},{12,8},{16,28},{20,16},{24,20},{28,24},{1,13},{... | collective-permute-start | bytes 393224 | tf_op jit(solution)/shard_map/ppermute | solution.py:212
  126.0 3.3 %collective-permute-done.7.refs_1_ = bf16[2,128,256]{2,1,0:T(8,128)(2,1)S(1)} collective-permute-done((bf16[2,128,256]{2,1,0:T(8,128)(2,1)}, bf16[2,128,256]{2,1,0:T(8,128)(2,1)S(1)}, u32[]{:S(2)}, u32[]{:S(2)}) %collective-permute-start.7) | collective-permute-done | bytes 131104 | tf_op jit(solution)/shard_map/ppermute | solution.py:212
  129.2 1.2 collective-permute-start.8
  130.4 7.4 %collective-permute-done.8.refs_2_ = bf16[2,128,256]{2,1,0:T(8,128)(2,1)S(1)} collective-permute-done((bf16[2,128,256]{2,1,0:T(8,128)(2,1)}, bf16[2,128,256]{2,1,0:T(8,128)(2,1)S(1)}, u32[]{:S(2)}, u32[]{:S(2)}) %collective-permute-start.8) | collective-permute-done | bytes 131104 | tf_op jit(solution)/shard_map/ppermute | solution.py:212
  137.9 1.4 collective-permute-start.25
  139.3 5.6 %collective-permute-done.9.refs_3_ = bf16[2,128,256]{2,1,0:T(8,128)(2,1)S(1)} collective-permute-done((bf16[2,128,256]{2,1,0:T(8,128)(2,1)}, bf16[2,128,256]{2,1,0:T(8,128)(2,1)S(1)}, u32[]{:S(2)}, u32[]{:S(2)}) %collective-permute-start.9) | collective-permute-done | bytes 131104 | tf_op jit(solution)/shard_map/ppermute | solution.py:212
  144.9 1.3 collective-permute-start.29
  146.8 0.7 collective-permute-start.33
  147.5 6.8 %collective-permute-done.25.refs_14_ = bf16[384,768]{1,0:T(8,128)(2,1)} collective-permute-done((bf16[384,768]{1,0:T(8,128)(2,1)S(1)}, bf16[384,768]{1,0:T(8,128)(2,1)}, u32[]{:S(2)}, u32[]{:S(2)}) %collective-permute-start.25) | collective-permute-done | bytes 589856 | tf_op jit(solution)/shard_map/ppermute | solution.py:235
  154.3 12.6 %collective-permute-done.29.refs_18_.refs_10_ = bf16[384,768]{1,0:T(8,128)(2,1)} collective-permute-done((bf16[384,768]{1,0:T(8,128)(2,1)S(1)}, bf16[384,768]{1,0:T(8,128)(2,1)}, u32[]{:S(2)}, u32[]{:S(2)}) %collective-permute-start.29) | collective-permute-done | bytes 589856 | tf_op jit(solution)/shard_map/ppermute | solution.py:235
  167.5 9.8 %collective-permute-done.33.refs_22_.refs_14_ = bf16[384,768]{1,0:T(8,128)(2,1)} collective-permute-done((bf16[384,768]{1,0:T(8,128)(2,1)S(1)}, bf16[384,768]{1,0:T(8,128)(2,1)}, u32[]{:S(2)}, u32[]{:S(2)}) %collective-permute-start.33) | collective-permute-done | bytes 589856 | tf_op jit(solution)/shard_map/ppermute | solution.py:235
  177.3 0.6 pad_add_fusion.where_ref
  177.9 4.4 %shard_map.59 = bf16[128,1536]{1,0:T(8,128)(2,1)} custom-call(s32[2]{0:T(128)} %pad_add_fusion.where_ref, bf16[2,128,256]{2,1,0:T(8,128)(2,1)} %get-tuple-element.37.refs_0_, bf16[2,128,256]{2,1,0:T(8,128)(2,1)} %copy-done.8, bf16[2,128,256]{2,1,0:T(8,128)(2,1)} %copy-done.9, bf16[2,128,256]{2,1,0:T(8,128)(2,1)} %copy-done.10, ...), custom_call_target="tpu_custom_call" | custom-call | tf_op jit(solution)/shard_map/pallas_call | solution.py:257
  182.4 4.4 %shard_map.60 = bf16[128,1536]{1,0:T(8,128)(2,1)} custom-call(s32[2]{0:T(128)} %pad_add_fusion.where_ref, bf16[2,128,256]{2,1,0:T(8,128)(2,1)} %get-tuple-element.37.refs_0_, bf16[2,128,256]{2,1,0:T(8,128)(2,1)} %copy-done.8, bf16[2,128,256]{2,1,0:T(8,128)(2,1)} %copy-done.9, bf16[2,128,256]{2,1,0:T(8,128)(2,1)} %copy-done.10, ...), custom_call_target="tpu_custom_call" | custom-call | tf_op jit(solution)/shard_map/pallas_call | solution.py:257
  186.8 2.0 collective-permute-start.36
  188.8 7.0 %shard_map.58.own_ref = f32[128,3072]{1,0:T(8,128)} custom-call(s32[2]{0:T(128)} %pad_add_fusion.where_ref, bf16[2,128,256]{2,1,0:T(8,128)(2,1)} %get-tuple-element.37.refs_0_, bf16[2,128,256]{2,1,0:T(8,128)(2,1)} %copy-done.8, bf16[2,128,256]{2,1,0:T(8,128)(2,1)} %copy-done.9, bf16[2,128,256]{2,1,0:T(8,128)(2,1)} %copy-done.10, ...), custom_call_target="tpu_custom_call" | custom-call | tf_op jit(solution)/shard_map/pallas_call | solution.py:257
  195.8 6.7 %collective-permute-done.36.refs_1_ = bf16[128,1536]{1,0:T(8,128)(2,1)S(1)} collective-permute-done((bf16[128,1536]{1,0:T(8,128)(2,1)}, bf16[128,1536]{1,0:T(8,128)(2,1)S(1)}, u32[]{:S(2)}, u32[]{:S(2)}) %collective-permute-start.36) | collective-permute-done | bytes 393248 | tf_op jit(solution)/shard_map/ppermute | solution.py:212
  202.5 0.8 copy-done.14
  203.3 2.6 %shard_map.61 = bf16[128,3072]{1,0:T(8,128)(2,1)} custom-call(s32[2]{0:T(128)} %pad_add_fusion.where_ref, f32[128,3072]{1,0:T(8,128)} %shard_map.58.own_ref, bf16[128,1536]{1,0:T(8,128)(2,1)} %copy-done.13, bf16[128,1536]{1,0:T(8,128)(2,1)} %copy-done.14), custom_call_target="tpu_custom_call" | custom-call | tf_op jit(solution)/shard_map/pallas_call | solution.py:276
  (94 shorter events, 3.1 us)
Async XLA Ops:
  4.0 9.7 %collective-permute-start.10 = (bf16[3,128,128]{2,1,0:T(8,128)(2,1)}, bf16[3,128,128]{2,1,0:T(8,128)(2,1)S(1)}, u32[]{:S(2)}, u32[]{:S(2)}) collective-permute-start(bf16[3,128,128]{2,1,0:T(8,128)(2,1)} %get-tuple-element.42), channel_id=1, source_target_pairs={{0,4},{4,8},{8,12},{12,0},{16,20},{20,24},{24,28},{28,16},{1,5},{5... | collective-permute-start | bytes 294920 | tf_op jit(solution)/shard_map/ppermute | solution.py:212
  7.1 90.1 %collective-permute-start.27 = (bf16[384,768]{1,0:T(8,128)(2,1)S(1)}, bf16[384,768]{1,0:T(8,128)(2,1)S(1)}, u32[]{:S(2)}, u32[]{:S(2)}) collective-permute-start(bf16[384,768]{1,0:T(8,128)(2,1)S(1)} %copy-done), channel_id=1, source_target_pairs={{0,8},{4,12},{8,0},{12,4},{1,9},{5,13},{9,1},{13,5},{2,10},{6,14},... | collective-permute-start | bytes 1769480 | tf_op jit(solution)/shard_map/ppermute | solution.py:225
  9.7 34.1 %collective-permute-start.11 = (bf16[3,128,128]{2,1,0:T(8,128)(2,1)}, bf16[3,128,128]{2,1,0:T(8,128)(2,1)S(1)}, u32[]{:S(2)}, u32[]{:S(2)}) collective-permute-start(bf16[3,128,128]{2,1,0:T(8,128)(2,1)} %get-tuple-element.43), channel_id=1, source_target_pairs={{0,8},{4,12},{8,0},{12,4},{16,24},{20,28},{24,16},{28,20},{1,9},{5... | collective-permute-start | bytes 294920 | tf_op jit(solution)/shard_map/ppermute | solution.py:212
  10.0 34.4 %collective-permute-start.12 = (bf16[3,128,128]{2,1,0:T(8,128)(2,1)}, bf16[3,128,128]{2,1,0:T(8,128)(2,1)S(1)}, u32[]{:S(2)}, u32[]{:S(2)}) collective-permute-start(bf16[3,128,128]{2,1,0:T(8,128)(2,1)} %get-tuple-element.44), channel_id=1, source_target_pairs={{0,12},{4,0},{8,4},{12,8},{16,28},{20,16},{24,20},{28,24},{1,13},{... | collective-permute-start | bytes 294920 | tf_op jit(solution)/shard_map/ppermute | solution.py:212
  12.1 35.3 %collective-permute-start.13 = (bf16[3,128,128]{2,1,0:T(8,128)(2,1)}, bf16[3,128,128]{2,1,0:T(8,128)(2,1)S(1)}, u32[]{:S(2)}, u32[]{:S(2)}) collective-permute-start(bf16[3,128,128]{2,1,0:T(8,128)(2,1)} %get-tuple-element.45), channel_id=1, source_target_pairs={{0,16},{4,20},{8,24},{12,28},{16,0},{20,4},{24,8},{28,12},{1,17},{... | collective-permute-start | bytes 294920 | tf_op jit(solution)/shard_map/ppermute | solution.py:212
  13.8 42.1 %copy-start.22 = (bf16[3,128,128]{2,1,0:T(8,128)(2,1)}, bf16[3,128,128]{2,1,0:T(8,128)(2,1)S(1)}, u32[]{:S(2)}) copy-start(bf16[3,128,128]{2,1,0:T(8,128)(2,1)S(1)} %collective-permute-done.10.refs_1_) | copy-start | bytes 294916
  13.8 34.3 %collective-permute-start.14 = (bf16[3,128,128]{2,1,0:T(8,128)(2,1)}, bf16[3,128,128]{2,1,0:T(8,128)(2,1)S(1)}, u32[]{:S(2)}, u32[]{:S(2)}) collective-permute-start(bf16[3,128,128]{2,1,0:T(8,128)(2,1)} %get-tuple-element.46), channel_id=1, source_target_pairs={{0,20},{4,24},{8,28},{12,16},{16,4},{20,8},{24,12},{28,0},{1,21},{... | collective-permute-start | bytes 294920 | tf_op jit(solution)/shard_map/ppermute | solution.py:212
  43.8 12.1 %copy-start.23 = (bf16[3,128,128]{2,1,0:T(8,128)(2,1)}, bf16[3,128,128]{2,1,0:T(8,128)(2,1)S(1)}, u32[]{:S(2)}) copy-start(bf16[3,128,128]{2,1,0:T(8,128)(2,1)S(1)} %collective-permute-done.11.refs_2_) | copy-start | bytes 294916
  43.8 9.7 %collective-permute-start.15 = (bf16[3,128,128]{2,1,0:T(8,128)(2,1)}, bf16[3,128,128]{2,1,0:T(8,128)(2,1)S(1)}, u32[]{:S(2)}, u32[]{:S(2)}) collective-permute-start(bf16[3,128,128]{2,1,0:T(8,128)(2,1)} %get-tuple-element.47), channel_id=1, source_target_pairs={{0,24},{4,28},{8,16},{12,20},{16,8},{20,12},{24,0},{28,4},{1,25},{... | collective-permute-start | bytes 294920 | tf_op jit(solution)/shard_map/ppermute | solution.py:212
  44.4 11.5 %collective-permute-start.16 = (bf16[3,128,128]{2,1,0:T(8,128)(2,1)}, bf16[3,128,128]{2,1,0:T(8,128)(2,1)S(1)}, u32[]{:S(2)}, u32[]{:S(2)}) collective-permute-start(bf16[3,128,128]{2,1,0:T(8,128)(2,1)} %get-tuple-element.48), channel_id=1, source_target_pairs={{0,28},{4,16},{8,20},{12,24},{16,12},{20,0},{24,4},{28,8},{1,29},{... | collective-permute-start | bytes 294920 | tf_op jit(solution)/shard_map/ppermute | solution.py:212
  47.5 31.7 %collective-permute-start = (bf16[3,128,256]{2,1,0:T(8,128)(2,1)}, bf16[3,128,256]{2,1,0:T(8,128)(2,1)S(1)}, u32[]{:S(2)}, u32[]{:S(2)}) collective-permute-start(bf16[3,128,256]{2,1,0:T(8,128)(2,1)} %get-tuple-element.30), channel_id=1, source_target_pairs={{0,4},{4,8},{8,12},{12,0},{16,20},{20,24},{24,28},{28,16},{1,5},{5... | collective-permute-start | bytes 589832 | tf_op jit(solution)/shard_map/ppermute | solution.py:212
  48.0 32.9 %collective-permute-start.1 = (bf16[3,128,256]{2,1,0:T(8,128)(2,1)}, bf16[3,128,256]{2,1,0:T(8,128)(2,1)S(1)}, u32[]{:S(2)}, u32[]{:S(2)}) collective-permute-start(bf16[3,128,256]{2,1,0:T(8,128)(2,1)} %get-tuple-element.31), channel_id=1, source_target_pairs={{0,8},{4,12},{8,0},{12,4},{16,24},{20,28},{24,16},{28,20},{1,9},{5... | collective-permute-start | bytes 589832 | tf_op jit(solution)/shard_map/ppermute | solution.py:212
  61.3 10.5 %collective-permute-start.17 = (bf16[2,128,128]{2,1,0:T(8,128)(2,1)}, bf16[2,128,128]{2,1,0:T(8,128)(2,1)S(1)}, u32[]{:S(2)}, u32[]{:S(2)}) collective-permute-start(bf16[2,128,128]{2,1,0:T(8,128)(2,1)} %get-tuple-element.50), channel_id=1, source_target_pairs={{0,12},{4,0},{8,4},{12,8},{16,28},{20,16},{24,20},{28,24},{1,13},{... | collective-permute-start | bytes 196616 | tf_op jit(solution)/shard_map/ppermute | solution.py:212
  61.5 20.8 %collective-permute-start.2 = (bf16[3,128,256]{2,1,0:T(8,128)(2,1)}, bf16[3,128,256]{2,1,0:T(8,128)(2,1)S(1)}, u32[]{:S(2)}, u32[]{:S(2)}) collective-permute-start(bf16[3,128,256]{2,1,0:T(8,128)(2,1)} %get-tuple-element.32), channel_id=1, source_target_pairs={{0,12},{4,0},{8,4},{12,8},{16,28},{20,16},{24,20},{28,24},{1,13},{... | collective-permute-start | bytes 589832 | tf_op jit(solution)/shard_map/ppermute | solution.py:212
  71.9 25.4 %copy-start.11 = (bf16[2,128,128]{2,1,0:T(8,128)(2,1)}, bf16[2,128,128]{2,1,0:T(8,128)(2,1)S(1)}, u32[]{:S(2)}) copy-start(bf16[2,128,128]{2,1,0:T(8,128)(2,1)S(1)} %collective-permute-done.17.refs_5_) | copy-start | bytes 196612
  71.9 5.4 %collective-permute-start.18 = (bf16[2,128,128]{2,1,0:T(8,128)(2,1)}, bf16[2,128,128]{2,1,0:T(8,128)(2,1)S(1)}, u32[]{:S(2)}, u32[]{:S(2)}) collective-permute-start(bf16[2,128,128]{2,1,0:T(8,128)(2,1)} %get-tuple-element.51), channel_id=1, source_target_pairs={{0,8},{4,12},{8,0},{12,4},{16,24},{20,28},{24,16},{28,20},{1,9},{5... | collective-permute-start | bytes 196616 | tf_op jit(solution)/shard_map/ppermute | solution.py:212
  77.2 22.0 %copy-start.12 = (bf16[2,128,128]{2,1,0:T(8,128)(2,1)}, bf16[2,128,128]{2,1,0:T(8,128)(2,1)S(1)}, u32[]{:S(2)}) copy-start(bf16[2,128,128]{2,1,0:T(8,128)(2,1)S(1)} %collective-permute-done.18.refs_6_) | copy-start | bytes 196612
  77.2 18.4 %collective-permute-start.3 = (bf16[3,128,256]{2,1,0:T(8,128)(2,1)}, bf16[3,128,256]{2,1,0:T(8,128)(2,1)S(1)}, u32[]{:S(2)}, u32[]{:S(2)}) collective-permute-start(bf16[3,128,256]{2,1,0:T(8,128)(2,1)} %get-tuple-element.33), channel_id=1, source_target_pairs={{0,16},{4,20},{8,24},{12,28},{16,0},{20,4},{24,8},{28,12},{1,17},{... | collective-permute-start | bytes 589832 | tf_op jit(solution)/shard_map/ppermute | solution.py:212
  79.2 16.5 %collective-permute-start.4 = (bf16[3,128,256]{2,1,0:T(8,128)(2,1)}, bf16[3,128,256]{2,1,0:T(8,128)(2,1)S(1)}, u32[]{:S(2)}, u32[]{:S(2)}) collective-permute-start(bf16[3,128,256]{2,1,0:T(8,128)(2,1)} %get-tuple-element.34), channel_id=1, source_target_pairs={{0,20},{4,24},{8,28},{12,16},{16,4},{20,8},{24,12},{28,0},{1,21},{... | collective-permute-start | bytes 589832 | tf_op jit(solution)/shard_map/ppermute | solution.py:212
  80.9 16.3 %collective-permute-start.5 = (bf16[3,128,256]{2,1,0:T(8,128)(2,1)}, bf16[3,128,256]{2,1,0:T(8,128)(2,1)S(1)}, u32[]{:S(2)}, u32[]{:S(2)}) collective-permute-start(bf16[3,128,256]{2,1,0:T(8,128)(2,1)} %get-tuple-element.35), channel_id=1, source_target_pairs={{0,24},{4,28},{8,16},{12,20},{16,8},{20,12},{24,0},{28,4},{1,25},{... | collective-permute-start | bytes 589832 | tf_op jit(solution)/shard_map/ppermute | solution.py:212
  82.3 17.0 %copy-start.17 = (bf16[3,128,256]{2,1,0:T(8,128)(2,1)}, bf16[3,128,256]{2,1,0:T(8,128)(2,1)S(1)}, u32[]{:S(2)}) copy-start(bf16[3,128,256]{2,1,0:T(8,128)(2,1)S(1)} %collective-permute-done.2.refs_3_) | copy-start | bytes 589828
  82.3 17.0 %collective-permute-start.6 = (bf16[3,128,256]{2,1,0:T(8,128)(2,1)}, bf16[3,128,256]{2,1,0:T(8,128)(2,1)S(1)}, u32[]{:S(2)}, u32[]{:S(2)}) collective-permute-start(bf16[3,128,256]{2,1,0:T(8,128)(2,1)} %get-tuple-element.36), channel_id=1, source_target_pairs={{0,28},{4,16},{8,20},{12,24},{16,12},{20,0},{24,4},{28,8},{1,29},{... | collective-permute-start | bytes 589832 | tf_op jit(solution)/shard_map/ppermute | solution.py:212
  95.6 42.3 %collective-permute-start.23 = (bf16[384,768]{1,0:T(8,128)(2,1)S(1)}, bf16[384,768]{1,0:T(8,128)(2,1)S(1)}, u32[]{:S(2)}, u32[]{:S(2)}) collective-permute-start(bf16[384,768]{1,0:T(8,128)(2,1)S(1)} %copy-done), channel_id=1, source_target_pairs={{0,4},{4,0},{8,12},{12,8},{1,5},{5,1},{9,13},{13,9},{2,6},{6,2},{1... | collective-permute-start | bytes 1769480 | tf_op jit(solution)/shard_map/ppermute | solution.py:225
  95.6 50.5 %collective-permute-start.21 = (bf16[384,768]{1,0:T(8,128)(2,1)S(1)}, bf16[384,768]{1,0:T(8,128)(2,1)S(1)}, u32[]{:S(2)}, u32[]{:S(2)}) collective-permute-start(bf16[384,768]{1,0:T(8,128)(2,1)S(1)} %copy-done), channel_id=1, source_target_pairs={{0,2},{1,3},{2,0},{3,1},{4,6},{5,7},{6,4},{7,5},{8,10},{9,11},{10,... | collective-permute-start | bytes 1769480 | tf_op jit(solution)/shard_map/ppermute | solution.py:235
  97.2 49.0 %collective-permute-start.20 = (bf16[384,768]{1,0:T(8,128)(2,1)S(1)}, bf16[384,768]{1,0:T(8,128)(2,1)S(1)}, u32[]{:S(2)}, u32[]{:S(2)}) collective-permute-start(bf16[384,768]{1,0:T(8,128)(2,1)S(1)} %copy-done), channel_id=1, source_target_pairs={{0,1},{1,0},{2,3},{3,2},{4,5},{5,4},{6,7},{7,6},{8,9},{9,8},{10,11... | collective-permute-start | bytes 1769480 | tf_op jit(solution)/shard_map/ppermute | solution.py:235
  97.3 85.0 %copy-start.1 = (bf16[384,768]{1,0:T(8,128)(2,1)}, bf16[384,768]{1,0:T(8,128)(2,1)S(1)}, u32[]{:S(2)}) copy-start(bf16[384,768]{1,0:T(8,128)(2,1)S(1)} %collective-permute-done.27.refs_16_.refs_8_) | copy-start | bytes 1769476
  97.3 49.5 %collective-permute-start.31 = (bf16[384,768]{1,0:T(8,128)(2,1)S(1)}, bf16[384,768]{1,0:T(8,128)(2,1)S(1)}, u32[]{:S(2)}, u32[]{:S(2)}) collective-permute-start(bf16[384,768]{1,0:T(8,128)(2,1)S(1)} %collective-permute-done.27.refs_16_.refs_8_), channel_id=1, source_target_pairs={{0,4},{4,0},{8,12},{12,8},{1,5},{5,1},{9,13},{13,9},{2,6},{6,2},{1... | collective-permute-start | bytes 1769480 | tf_op jit(solution)/shard_map/ppermute | solution.py:225
  99.3 21.6 %collective-permute-start.19 = (bf16[2,128,128]{2,1,0:T(8,128)(2,1)}, bf16[2,128,128]{2,1,0:T(8,128)(2,1)}, u32[]{:S(2)}, u32[]{:S(2)}) collective-permute-start(bf16[2,128,128]{2,1,0:T(8,128)(2,1)} %get-tuple-element.52), channel_id=1, source_target_pairs={{0,4},{4,8},{8,12},{12,0},{16,20},{20,24},{24,28},{28,16},{1,5},{5... | collective-permute-start | bytes 196616 | tf_op jit(solution)/shard_map/ppermute | solution.py:212
  120.9 8.3 %collective-permute-start.7 = (bf16[2,128,256]{2,1,0:T(8,128)(2,1)}, bf16[2,128,256]{2,1,0:T(8,128)(2,1)S(1)}, u32[]{:S(2)}, u32[]{:S(2)}) collective-permute-start(bf16[2,128,256]{2,1,0:T(8,128)(2,1)} %get-tuple-element.38), channel_id=1, source_target_pairs={{0,12},{4,0},{8,4},{12,8},{16,28},{20,16},{24,20},{28,24},{1,13},{... | collective-permute-start | bytes 393224 | tf_op jit(solution)/shard_map/ppermute | solution.py:212
  129.2 16.9 %copy-start.8 = (bf16[2,128,256]{2,1,0:T(8,128)(2,1)}, bf16[2,128,256]{2,1,0:T(8,128)(2,1)S(1)}, u32[]{:S(2)}) copy-start(bf16[2,128,256]{2,1,0:T(8,128)(2,1)S(1)} %collective-permute-done.7.refs_1_) | copy-start | bytes 393220
  129.2 8.6 %collective-permute-start.8 = (bf16[2,128,256]{2,1,0:T(8,128)(2,1)}, bf16[2,128,256]{2,1,0:T(8,128)(2,1)S(1)}, u32[]{:S(2)}, u32[]{:S(2)}) collective-permute-start(bf16[2,128,256]{2,1,0:T(8,128)(2,1)} %get-tuple-element.39), channel_id=1, source_target_pairs={{0,8},{4,12},{8,0},{12,4},{16,24},{20,28},{24,16},{28,20},{1,9},{5... | collective-permute-start | bytes 393224 | tf_op jit(solution)/shard_map/ppermute | solution.py:212
  137.9 7.0 %collective-permute-start.9 = (bf16[2,128,256]{2,1,0:T(8,128)(2,1)}, bf16[2,128,256]{2,1,0:T(8,128)(2,1)S(1)}, u32[]{:S(2)}, u32[]{:S(2)}) collective-permute-start(bf16[2,128,256]{2,1,0:T(8,128)(2,1)} %get-tuple-element.40), channel_id=1, source_target_pairs={{0,4},{4,8},{8,12},{12,0},{16,20},{20,24},{24,28},{28,16},{1,5},{5... | collective-permute-start | bytes 393224 | tf_op jit(solution)/shard_map/ppermute | solution.py:212
  137.9 40.0 %copy-start.2 = (bf16[384,768]{1,0:T(8,128)(2,1)}, bf16[384,768]{1,0:T(8,128)(2,1)S(1)}, u32[]{:S(2)}) copy-start(bf16[384,768]{1,0:T(8,128)(2,1)S(1)} %collective-permute-done.23.refs_12_) | copy-start | bytes 1769476
  137.9 16.4 %collective-permute-start.25 = (bf16[384,768]{1,0:T(8,128)(2,1)S(1)}, bf16[384,768]{1,0:T(8,128)(2,1)}, u32[]{:S(2)}, u32[]{:S(2)}) collective-permute-start(bf16[384,768]{1,0:T(8,128)(2,1)S(1)} %collective-permute-done.23.refs_12_), channel_id=1, source_target_pairs={{0,2},{1,3},{2,0},{3,1},{4,6},{5,7},{6,4},{7,5},{8,10},{9,11},{10,... | collective-permute-start | bytes 1769480 | tf_op jit(solution)/shard_map/ppermute | solution.py:235
  144.9 22.1 %collective-permute-start.29 = (bf16[384,768]{1,0:T(8,128)(2,1)S(1)}, bf16[384,768]{1,0:T(8,128)(2,1)}, u32[]{:S(2)}, u32[]{:S(2)}) collective-permute-start(bf16[384,768]{1,0:T(8,128)(2,1)S(1)} %collective-permute-done.27.refs_16_.refs_8_), channel_id=1, source_target_pairs={{0,2},{1,3},{2,0},{3,1},{4,6},{5,7},{6,4},{7,5},{8,10},{9,11},{10,... | collective-permute-start | bytes 1769480 | tf_op jit(solution)/shard_map/ppermute | solution.py:235
  146.2 31.7 %copy-start.3 = (bf16[384,768]{1,0:T(8,128)(2,1)}, bf16[384,768]{1,0:T(8,128)(2,1)S(1)}, u32[]{:S(2)}) copy-start(bf16[384,768]{1,0:T(8,128)(2,1)S(1)} %collective-permute-done.21.refs_10_) | copy-start | bytes 1769476
  146.2 20.7 %collective-permute-start.24 = (bf16[384,768]{1,0:T(8,128)(2,1)S(1)}, bf16[384,768]{1,0:T(8,128)(2,1)S(1)}, u32[]{:S(2)}, u32[]{:S(2)}) collective-permute-start(bf16[384,768]{1,0:T(8,128)(2,1)S(1)} %collective-permute-done.23.refs_12_), channel_id=1, source_target_pairs={{0,1},{1,0},{2,3},{3,2},{4,5},{5,4},{6,7},{7,6},{8,9},{9,8},{10,11... | collective-permute-start | bytes 1769480 | tf_op jit(solution)/shard_map/ppermute | solution.py:235
  146.3 31.6 %copy-start.4 = (bf16[384,768]{1,0:T(8,128)(2,1)}, bf16[384,768]{1,0:T(8,128)(2,1)S(1)}, u32[]{:S(2)}) copy-start(bf16[384,768]{1,0:T(8,128)(2,1)S(1)} %collective-permute-done.20.refs_9_) | copy-start | bytes 1769476
  146.3 21.1 %collective-permute-start.22 = (bf16[384,768]{1,0:T(8,128)(2,1)S(1)}, bf16[384,768]{1,0:T(8,128)(2,1)S(1)}, u32[]{:S(2)}, u32[]{:S(2)}) collective-permute-start(bf16[384,768]{1,0:T(8,128)(2,1)S(1)} %collective-permute-done.21.refs_10_), channel_id=1, source_target_pairs={{0,1},{1,0},{2,3},{3,2},{4,5},{5,4},{6,7},{7,6},{8,9},{9,8},{10,11... | collective-permute-start | bytes 1769480 | tf_op jit(solution)/shard_map/ppermute | solution.py:235
  146.8 35.5 %copy-start.5 = (bf16[384,768]{1,0:T(8,128)(2,1)}, bf16[384,768]{1,0:T(8,128)(2,1)S(1)}, u32[]{:S(2)}) copy-start(bf16[384,768]{1,0:T(8,128)(2,1)S(1)} %collective-permute-done.31.refs_20_.refs_12_) | copy-start | bytes 1769476
  146.8 30.5 %collective-permute-start.33 = (bf16[384,768]{1,0:T(8,128)(2,1)S(1)}, bf16[384,768]{1,0:T(8,128)(2,1)}, u32[]{:S(2)}, u32[]{:S(2)}) collective-permute-start(bf16[384,768]{1,0:T(8,128)(2,1)S(1)} %collective-permute-done.31.refs_20_.refs_12_), channel_id=1, source_target_pairs={{0,2},{1,3},{2,0},{3,1},{4,6},{5,7},{6,4},{7,5},{8,10},{9,11},{10,... | collective-permute-start | bytes 1769480 | tf_op jit(solution)/shard_map/ppermute | solution.py:235
  154.3 23.6 %collective-permute-start.26 = (bf16[384,768]{1,0:T(8,128)(2,1)}, bf16[384,768]{1,0:T(8,128)(2,1)}, u32[]{:S(2)}, u32[]{:S(2)}) collective-permute-start(bf16[384,768]{1,0:T(8,128)(2,1)} %collective-permute-done.25.refs_14_), channel_id=1, source_target_pairs={{0,1},{1,0},{2,3},{3,2},{4,5},{5,4},{6,7},{7,6},{8,9},{9,8},{10,11... | collective-permute-start | bytes 1769480 | tf_op jit(solution)/shard_map/ppermute | solution.py:235
  166.9 15.5 %collective-permute-start.28 = (bf16[384,768]{1,0:T(8,128)(2,1)S(1)}, bf16[384,768]{1,0:T(8,128)(2,1)}, u32[]{:S(2)}, u32[]{:S(2)}) collective-permute-start(bf16[384,768]{1,0:T(8,128)(2,1)S(1)} %collective-permute-done.27.refs_16_.refs_8_), channel_id=1, source_target_pairs={{0,1},{1,0},{2,3},{3,2},{4,5},{5,4},{6,7},{7,6},{8,9},{9,8},{10,11... | collective-permute-start | bytes 1769480 | tf_op jit(solution)/shard_map/ppermute | solution.py:235
  166.9 15.5 %collective-permute-start.32 = (bf16[384,768]{1,0:T(8,128)(2,1)S(1)}, bf16[384,768]{1,0:T(8,128)(2,1)}, u32[]{:S(2)}, u32[]{:S(2)}) collective-permute-start(bf16[384,768]{1,0:T(8,128)(2,1)S(1)} %collective-permute-done.31.refs_20_.refs_12_), channel_id=1, source_target_pairs={{0,1},{1,0},{2,3},{3,2},{4,5},{5,4},{6,7},{7,6},{8,9},{9,8},{10,11... | collective-permute-start | bytes 1769480 | tf_op jit(solution)/shard_map/ppermute | solution.py:235
  167.4 15.0 %collective-permute-start.30 = (bf16[384,768]{1,0:T(8,128)(2,1)}, bf16[384,768]{1,0:T(8,128)(2,1)}, u32[]{:S(2)}, u32[]{:S(2)}) collective-permute-start(bf16[384,768]{1,0:T(8,128)(2,1)} %collective-permute-done.29.refs_18_.refs_10_), channel_id=1, source_target_pairs={{0,1},{1,0},{2,3},{3,2},{4,5},{5,4},{6,7},{7,6},{8,9},{9,8},{10,11... | collective-permute-start | bytes 1769480 | tf_op jit(solution)/shard_map/ppermute | solution.py:235
  177.3 5.1 %collective-permute-start.34 = (bf16[384,768]{1,0:T(8,128)(2,1)}, bf16[384,768]{1,0:T(8,128)(2,1)}, u32[]{:S(2)}, u32[]{:S(2)}) collective-permute-start(bf16[384,768]{1,0:T(8,128)(2,1)} %collective-permute-done.33.refs_22_.refs_14_), channel_id=1, source_target_pairs={{0,1},{1,0},{2,3},{3,2},{4,5},{5,4},{6,7},{7,6},{8,9},{9,8},{10,11... | collective-permute-start | bytes 1769480 | tf_op jit(solution)/shard_map/ppermute | solution.py:235
  182.3 13.5 %collective-permute-start.35 = (bf16[128,1536]{1,0:T(8,128)(2,1)}, bf16[128,1536]{1,0:T(8,128)(2,1)S(1)}, u32[]{:S(2)}, u32[]{:S(2)}) collective-permute-start(bf16[128,1536]{1,0:T(8,128)(2,1)} %shard_map.59), channel_id=1, source_target_pairs={{0,16},{4,20},{8,24},{12,28},{16,0},{20,4},{24,8},{28,12},{1,17},{... | collective-permute-start | bytes 1179656 | tf_op jit(solution)/shard_map/ppermute | solution.py:212
  186.8 15.7 %collective-permute-start.36 = (bf16[128,1536]{1,0:T(8,128)(2,1)}, bf16[128,1536]{1,0:T(8,128)(2,1)S(1)}, u32[]{:S(2)}, u32[]{:S(2)}) collective-permute-start(bf16[128,1536]{1,0:T(8,128)(2,1)} %shard_map.60), channel_id=1, source_target_pairs={{0,16},{4,20},{8,24},{12,28},{16,0},{20,4},{24,8},{28,12},{1,17},{... | collective-permute-start | bytes 1179656 | tf_op jit(solution)/shard_map/ppermute | solution.py:212
  (18 other events, 94.3 us)
